TPU v7x, 512 devices: a whole 4x8x8 slice. The times are simulated.
512 devices in a mesh: dp: 32 (over x, z), patch: 16 (over y, core).
Axes of the slice: x: 4, y: 8, z: 8, core: 2. Of those that a mesh axis runs over, the one named last changes fastest.
Arguments:
- query_rows: bfloat16 [32, 2048, 576], P('dp', 'patch'), may hold values from -6 to 6
- key_rows: bfloat16 [32, 2048, 576], P('dp', 'patch'), may hold values from -6 to 6
- value_rows: bfloat16 [32, 2048, 576], P('dp', 'patch'), may hold values from -6 to 6
- out_weight: bfloat16 [576, 1152], replicated, may hold values from -0.25 to 0.25
- target: bfloat16 [32, 2048, 1152], P('dp', 'patch'), may hold values from -6 to 6
- lengths: int32 [32], P('dp'), may hold values from 256 to 2048
- segments: int32 [32, 2048], P('dp', 'patch'), may hold values from 0 to 7, never falling along the last dimension, each value on 1 to 1024 neighbouring positions
Outputs:
- query_grad: float32 [32, 2048, 576], P('dp', 'patch')
- key_grad: float32 [32, 2048, 576], P('dp', 'patch')
- value_grad: float32 [32, 2048, 576], P('dp', 'patch')
- weight_grad: float32 [576, 1152], P('patch', 'dp')
- loss: float32 [], replicated
All inputs are finite; a program needn't handle non-finite values.
Results may differ from a plain program's by a relative error of at most 0.024.
Values may be sent and summed in bfloat16 or wider, within the bound.
No kernel may reach another device: no remote copies, remote signals or barrier semaphores. Data moves between devices by JAX's collectives and lax.ppermute only.
A program may use at most 64 MiB of HBM per device.

v0:
```python
import math

import jax
import jax.numpy as jnp
from jax import lax
from jax.sharding import Mesh
from jax.sharding import PartitionSpec as P

WIDTH = 1152
HEADS = 8
HEAD_DIM = 72
FEAT = 576
PATCH = ("patch_0", "patch_1")
DP = ("dp_0", "dp_1")
DP_PATCH = ("dp_0", "dp_1", "patch_0", "patch_1")


NEG_LARGE = -1e30


def from_everyone(value, axis):
    copies = jnp.broadcast_to(value, (lax.axis_size(axis), *value.shape))
    return lax.all_to_all(copies, axis, split_axis=0, concat_axis=0, tiled=True)


def of_everyone(value, axis):
    return from_everyone(value, axis).sum(axis=0)


def sent_together(arrays, axis, dim, along):
    ends, at = ([], 0)
    for a in arrays[:-1]:
        at += a.shape[along]
        ends.append(at)
    both = jnp.concatenate(arrays, axis=along)
    return tuple(jnp.split(lax.all_gather(both, axis, axis=dim, tiled=True), ends, axis=along))


def by_axis(value, axes):
    for axis in axes:
        value = lax.psum(value, axis)
    return value


def in_blocks(value, dim, peers):
    shape = value.shape
    pieces = value.reshape(*shape[:dim], peers, shape[dim] // peers, *shape[dim + 1 :])
    return jnp.moveaxis(pieces, dim, 0)


def sum_at_owner(value, axis, dim):
    peers = lax.axis_size(axis)
    pieces = lax.all_to_all(in_blocks(value, dim, peers), axis, 0, 0, tiled=True)
    return jnp.sum(pieces.astype(jnp.float32), axis=0)


def head_view(rows):
    return rows.reshape(rows.shape[0], HEADS, HEAD_DIM)


def pair_mask(query_group, key_group):
    return (query_group[:, None] == key_group[None, :])[None, :, :]


def forward_block(running, query_heads, own_group, group_all, pieces):
    run_max, run_denom, run_accum = running
    score_scale = 1.0 / math.sqrt(HEAD_DIM)
    key_heads = head_view(pieces[0][0])
    value_heads = head_view(pieces[1][0])
    allowed = pair_mask(own_group, group_all)
    scores = (
        jnp.einsum("qhe,khe->hqk", query_heads, key_heads, preferred_element_type=jnp.float32)
        * score_scale
    )
    masked = jnp.where(allowed, scores, NEG_LARGE)
    new_max = jnp.maximum(run_max, jnp.max(masked, axis=2))
    probs = jnp.where(allowed, jnp.exp(masked - new_max[:, :, None]), 0.0)
    shrink = jnp.exp(run_max - new_max)
    run_denom = jnp.sum(probs, axis=2)
    added = jnp.einsum(
        "hqk,khe->qhe", probs.astype(jnp.bfloat16), value_heads, preferred_element_type=jnp.float32
    )
    run_accum = run_accum * shrink.T[:, :, None] + added
    return (new_max, run_denom, run_accum)


def query_grad_block(query_heads, grad_heads, log_norm, delta, own_group, group_all, pieces):
    score_scale = 1.0 / math.sqrt(HEAD_DIM)
    key_heads = head_view(pieces[0][0])
    value_heads = head_view(pieces[1][0])
    allowed = pair_mask(own_group, group_all)
    scores = (
        jnp.einsum("qhe,khe->hqk", query_heads, key_heads, preferred_element_type=jnp.float32)
        * score_scale
    )
    masked = jnp.where(allowed, scores, NEG_LARGE)
    probs = jnp.where(allowed, jnp.exp(masked - log_norm[:, :, None]), 0.0)
    dprobs = jnp.einsum("qhe,khe->hqk", grad_heads, value_heads, preferred_element_type=jnp.float32)
    dscores = (probs * (dprobs - delta[:, :, None])).astype(jnp.bfloat16)
    return (
        jnp.einsum("hqk,khe->qhe", dscores, key_heads, preferred_element_type=jnp.float32)
        * score_scale
    )


def key_grad_block(own_keys, own_values, own_group, group_all, log_all, delta_all, pieces):
    score_scale = 1.0 / math.sqrt(HEAD_DIM)
    query_heads = head_view(pieces[0][0])
    grad_heads = head_view(pieces[1][0])
    allowed = pair_mask(group_all, own_group)
    scores = (
        jnp.einsum("qhe,khe->hqk", query_heads, own_keys, preferred_element_type=jnp.float32)
        * score_scale
    )
    masked = jnp.where(allowed, scores, NEG_LARGE)
    probs = jnp.where(allowed, jnp.exp(masked - log_all[:, :, None]), 0.0)
    grad_values = jnp.einsum(
        "hqk,qhe->khe", probs.astype(jnp.bfloat16), grad_heads, preferred_element_type=jnp.float32
    )
    dprobs = jnp.einsum("qhe,khe->hqk", grad_heads, own_values, preferred_element_type=jnp.float32)
    dscores = (probs * (dprobs - delta_all[:, :, None])).astype(jnp.bfloat16)
    grad_keys = (
        jnp.einsum("hqk,qhe->khe", dscores, query_heads, preferred_element_type=jnp.float32)
        * score_scale
    )
    return (grad_keys, grad_values)


def local(query_rows, key_rows, value_rows, out_weight, target, lengths, segments):
    own_rows = query_rows.shape[1]
    members = lax.axis_size(PATCH)
    groups = lax.axis_size(DP)
    total_rows = own_rows * members
    length = lengths[0]
    count = of_everyone(length.astype(jnp.float32), DP)
    offset = lax.axis_index(PATCH) * own_rows
    own_live = offset + lax.iota(jnp.int32, own_rows) < length
    segment_all = lax.all_gather(segments, PATCH, axis=1, tiled=True)
    group_all = jnp.where(lax.iota(jnp.int32, total_rows) < length, segment_all[0], -1)
    own_group = lax.dynamic_slice_in_dim(group_all, offset, own_rows, 0)
    query_heads = head_view(query_rows[0])
    starting = (
        jnp.full((HEADS, own_rows), NEG_LARGE, jnp.float32),
        jnp.zeros((HEADS, own_rows), jnp.float32),
        jnp.zeros((own_rows, HEADS, HEAD_DIM), jnp.float32),
    )
    forward_state = forward_block(
        starting,
        query_heads,
        own_group,
        group_all,
        sent_together((key_rows, value_rows), PATCH, 1, 0),
    )
    run_max, run_denom, run_accum = forward_state
    log_norm = run_max + jnp.log(run_denom)
    attn = (run_accum / run_denom.T[:, :, None]).reshape(own_rows, FEAT).astype(jnp.bfloat16)
    output = jnp.dot(attn, out_weight, preferred_element_type=jnp.float32)
    error = jnp.where(own_live[:, None], output - target[0].astype(jnp.float32), 0.0)
    loss_part = jnp.sum(error * error)
    grad_out = (2.0 * error).astype(jnp.bfloat16)
    weight_part = jnp.einsum("tf,td->fd", attn, grad_out, preferred_element_type=jnp.float32)
    grad_attn = jnp.einsum(
        "td,fd->tf", grad_out, out_weight, preferred_element_type=jnp.float32
    ).astype(jnp.bfloat16)
    delta = jnp.sum(
        (grad_attn.astype(jnp.float32) * attn.astype(jnp.float32)).reshape(
            own_rows, HEADS, HEAD_DIM
        ),
        axis=2,
    ).T
    grad_heads = head_view(grad_attn)
    query_raw = query_grad_block(
        query_heads,
        grad_heads,
        log_norm,
        delta,
        own_group,
        group_all,
        sent_together((key_rows, value_rows), PATCH, 1, 0),
    )
    log_all, delta_all = sent_together((log_norm, delta), PATCH, 1, 0)
    own_keys = head_view(key_rows[0])
    own_values = head_view(value_rows[0])
    key_raw, value_raw = key_grad_block(
        own_keys,
        own_values,
        own_group,
        group_all,
        log_all,
        delta_all,
        sent_together((query_rows, grad_attn[None]), PATCH, 1, 0),
    )
    loss_total = by_axis(loss_part, DP_PATCH)
    row_share = sum_at_owner(weight_part.astype(jnp.bfloat16), PATCH, 0)
    weight_share = sum_at_owner(row_share.astype(jnp.bfloat16), DP, 1)
    ratio = jnp.float32(groups * total_rows) / count
    query_grad = (ratio * query_raw).reshape(1, own_rows, FEAT)
    key_grad = (ratio * key_raw).reshape(1, own_rows, FEAT)
    value_grad = (ratio * value_raw).reshape(1, own_rows, FEAT)
    weight_grad = weight_share * (ratio / total_rows)
    loss = loss_total / (count * WIDTH)
    return (query_grad, key_grad, value_grad, weight_grad, loss)


def solution(mesh):
    torus = Mesh(mesh.devices.reshape(4, 8, 8, 2), ("dp_0", "dp_1", "patch_0", "patch_1"))
    return jax.shard_map(
        local,
        mesh=torus,
        in_specs=(
            P(DP, PATCH, None),
            P(DP, PATCH, None),
            P(DP, PATCH, None),
            P(),
            P(DP, PATCH, None),
            P(DP),
            P(DP, PATCH),
        ),
        out_specs=(P(DP, PATCH, None), P(DP, PATCH, None), P(DP, PATCH, None), P(PATCH, DP), P()),
        check_vma=False,
    )
```

profile of v0, /device:TPU:1, one launch (start us, length us, event | category | flops | bytes accessed | tf_op | source)
XLA Modules:
  0.0 233.7 jit_solution(14534418018708874223)
XLA Ops:
  7.2 1.8 pad_maximum_fusion
  9.8 21.1 %all_gather.14 = s32[1,2048]{1,0:T(1,128)S(1)} all-gather(s32[1,128]{1,0:T(1,128)} %param.13), channel_id=1, replica_groups=mesh['dp_0'=4,'dp_1'=8,'patch_0'=8,'patch_1'=2] {'patch_0','patch_1'}, dimensions={1}, use_global_device_ids=true | all-gather | bytes 8704 | tf_op jit(solution)/shard_map/all_gather | solution.py:138
  31.3 40.1 %all-gather.3.cloned.1.call-done = bf16[2,2048,576]{1,2,0:T(8,128)(2,1)} async-done(((bf16[2,128,576]{1,2,0:T(8,128)(2,1)}), bf16[2,2048,576]{1,2,0:T(8,128)(2,1)}) %all-gather.3.cloned.1.call-update) | async-done | bytes 4718608 | tf_op jit(solution)/shard_map/all_gather | solution.py:36
  71.4 2.8 %fusion.46 = (bf16[1,2048,576]{1,2,0:T(8,128)(2,1)S(1)}, bf16[1,2048,576]{1,2,0:T(8,128)(2,1)S(1)}) fusion(bf16[2,2048,576]{1,2,0:T(8,128)(2,1)} %all-gather.3.cloned.1.call-done), kind=kLoop, calls=%fused_computation.58 | loop fusion | bytes 9437184 | tf_op jit(solution)/shard_map/split | solution.py:36
  74.2 2.2 fusion.3
  76.3 2.0 fusion.1
  78.4 2.9 %fusion.27 = bf16[128,8,72]{0,2,1:T(8,128)(2,1)S(1)} fusion(bf16[2048,8,72]{0,2,1:T(8,128)(2,1)S(1)} %bitcast.87, f32[8,2048,128]{2,1,0:T(8,128)S(1)} %get-tuple-element.14, f32[8,128]{1,0:T(8,128)S(1)} %broadcast_maximum_fusion, pred[128,2048]{0,1:T(8,128)(4,1)S(1)} %broadcast_compare_fusion.1, f32[128,8]{0,1:T(8,128)S(1)} %bitcast.102, ...), kind=kOutput, calls=%fused_computation.25 | convolution fusion | flops 312696832 | bytes 11169792 | tf_op jit(solution)/shard_map/hqk,khe->qhe/dot_general | solution.py:80
  81.4 1.1 multiply_reduce_fusion
  82.5 1.2 convert_multiply_fusion
  83.7 0.8 pad_maximum_fusion.1
  85.1 8.3 %all-to-all-start = ((f32[32,1,1]{2,1,0:T(1,128)}), f32[32,1,1]{2,1,0:T(1,128)S(1)}, u32[]{:S(2)}, u32[]{:S(2)}) async-start(f32[32,1,1]{2,1,0:T(1,128)} %broadcast_in_dim.100), calls=%async_computation | async-start | bytes 32768 | tf_op jit(solution)/shard_map/all_to_all | solution.py:23
  93.4 1.4 convolution_convert_fusion
  94.8 1.3 reshape.133
  96.1 5.9 %all-to-all-done = f32[32,1,1]{2,1,0:T(1,128)S(1)} async-done(((f32[32,1,1]{2,1,0:T(1,128)}), f32[32,1,1]{2,1,0:T(1,128)S(1)}, u32[]{:S(2)}, u32[]{:S(2)}) %all-to-all-start) | async-done | bytes 160 | tf_op jit(solution)/shard_map/all_to_all | solution.py:23
  102.0 6.7 %all-to-all-start.1 = ((bf16[16,36,1152]{2,1,0:T(8,128)(2,1)}), bf16[16,36,1152]{2,1,0:T(8,128)(2,1)S(1)}, u32[]{:S(2)}, u32[]{:S(2)}) async-start(bf16[16,36,1152]{2,1,0:T(8,128)(2,1)} %reshape.133), calls=%async_computation.1 | async-start | bytes 2949120 | tf_op jit(solution)/shard_map/all_to_all | solution.py:53
  108.8 1.0 broadcast_compare_fusion
  109.8 0.6 reduce_sum.59
  111.1 8.2 %psum.28 = f32[]{:T(128)} all-reduce(f32[]{:T(128)} %get-tuple-element.17), channel_id=1, replica_groups=mesh['dp_0'=4,'dp_1'=8,'patch_0'=8,'patch_1'=2] {'dp_0'}, use_global_device_ids=true, to_apply=%region_7.8 | all-reduce | flops 1 | bytes 8 | tf_op jit(solution)/shard_map/psum | solution.py:41
  119.3 13.3 %psum.29 = f32[]{:T(128)} all-reduce(f32[]{:T(128)} %psum.28), channel_id=1, replica_groups=mesh['dp_0'=4,'dp_1'=8,'patch_0'=8,'patch_1'=2] {'dp_1'}, use_global_device_ids=true, to_apply=%region_8.9 | all-reduce | flops 1 | bytes 8 | tf_op jit(solution)/shard_map/psum | solution.py:41
  133.3 30.3 %psum.30 = f32[]{:T(128)} all-reduce(f32[]{:T(128)} %psum.29), channel_id=1, replica_groups=mesh['dp_0'=4,'dp_1'=8,'patch_0'=8,'patch_1'=2] {'patch_0'}, use_global_device_ids=true, to_apply=%region_9.10 | all-reduce | flops 1 | bytes 8 | tf_op jit(solution)/shard_map/psum | solution.py:41
  163.6 1.0 reduce_sum.58
  164.6 17.3 %all_gather.16 = f32[16,2048]{1,0:T(8,128)S(1)} all-gather(f32[16,128]{1,0:T(8,128)S(1)} %pad_maximum_fusion.2), channel_id=1, replica_groups=mesh['dp_0'=4,'dp_1'=8,'patch_0'=8,'patch_1'=2] {'patch_0','patch_1'}, dimensions={1}, use_global_device_ids=true | all-gather | bytes 139264 | tf_op jit(solution)/shard_map/all_gather | solution.py:36
  182.0 9.7 %fusion.20 = f32[8,72,128]{2,1,0:T(8,128)} fusion(bf16[2048,8,72]{0,2,1:T(8,128)(2,1)} %bitcast.84, f32[8,2048,128]{2,1,0:T(8,128)} %copy-done.1, bf16[128,8,72]{0,2,1:T(8,128)(2,1)} %bitcast.96, bf16[2048,8,72]{0,2,1:T(8,128)(2,1)} %bitcast.88, f32[8,128]{1,0:T(8,128)S(1)} %bitcast.104, f32[8,128]{1,0:T(8,128)S(1)} %get-tuple-element.11, ...), kind=kOutput, calls=%fused_computation.21 | convolution fusion | flops 618733568 | bytes 13819908 | tf_op jit(solution)/shard_map/hqk,khe->qhe/dot_general | solution.py:101
  192.0 0.8 reshape.134
  192.9 1.0 reshape.136
  193.9 3.9 %all-to-all-start.2 = ((bf16[32,2,648]{2,1,0:T(2,128)(2,1)}), bf16[32,2,648]{2,1,0:T(2,128)(2,1)S(1)}, u32[]{:S(2)}, u32[]{:S(2)}) async-start(bf16[32,2,648]{2,1,0:T(2,128)(2,1)} %reshape.136), calls=%async_computation.2 | async-start | bytes 196608 | tf_op jit(solution)/shard_map/all_to_all | solution.py:53
  197.8 3.3 %psum.31 = f32[]{:T(128)} all-reduce(f32[]{:T(128)} %psum.30), channel_id=1, replica_groups=mesh['dp_0'=4,'dp_1'=8,'patch_0'=8,'patch_1'=2] {'patch_1'}, use_global_device_ids=true, to_apply=%region_10.11 | all-reduce | flops 1 | bytes 8 | tf_op jit(solution)/shard_map/psum | solution.py:41
  201.8 5.0 %all-to-all-done.2 = bf16[32,2,648]{2,1,0:T(2,128)(2,1)S(1)} async-done(((bf16[32,2,648]{2,1,0:T(2,128)(2,1)}), bf16[32,2,648]{2,1,0:T(2,128)(2,1)S(1)}, u32[]{:S(2)}, u32[]{:S(2)}) %all-to-all-start.2) | async-done | bytes 82976 | tf_op jit(solution)/shard_map/all_to_all | solution.py:53
  207.9 2.8 %fusion.45 = (bf16[1,2048,576]{1,2,0:T(8,128)(2,1)S(1)}, bf16[1,2048,576]{1,2,0:T(8,128)(2,1)S(1)}) fusion(bf16[2,2048,576]{1,2,0:T(8,128)(2,1)} %all-gather.5.cloned.1.call-done), kind=kLoop, calls=%fused_computation.57 | loop fusion | bytes 9437184 | tf_op jit(solution)/shard_map/split | solution.py:36
  210.7 1.5 fusion.48
  212.2 3.9 %fusion.21 = f32[8,72,128]{2,1,0:T(8,128)} fusion(bf16[2048,8,72]{0,2,1:T(8,128)(2,1)S(1)} %bitcast.89, f32[8,2048,128]{2,1,0:T(8,128)S(1)} %fusion.48, f32[8,2048]{1,0:T(8,128)S(1)} %get-tuple-element.9, pred[2048,128]{1,0:T(8,128)(4,1)S(1)} %copy-done.12, f32[]{:T(128)S(6)} %div.19), kind=kOutput, calls=%fused_computation.22 | convolution fusion | flops 312549376 | bytes 11370500 | tf_op jit(solution)/shard_map/hqk,qhe->khe/dot_general | solution.py:117
  216.1 9.6 %fusion.19 = f32[8,72,128]{2,1,0:T(8,128)} fusion(bf16[2048,8,72]{0,2,1:T(8,128)(2,1)} %bitcast.86, f32[8,2048,128]{2,1,0:T(8,128)} %copy-done.4, bf16[2048,8,72]{0,2,1:T(8,128)(2,1)} %bitcast.90, bf16[128,8,72]{0,2,1:T(8,128)(2,1)S(1)} %bitcast.99, f32[8,2048]{1,0:T(8,128)S(1)} %get-tuple-element.10, f32[8,2048]{1,0:T(8,128)S(1)} %get-tuple-element.9, ...), kind=kOutput, calls=%fused_computation.20 | convolution fusion | flops 618733568 | bytes 13942788 | tf_op jit(solution)/shard_map/hqk,qhe->khe/dot_general | solution.py:123
  (49 shorter events, 2.7 us)
Async XLA Ops:
  7.2 74.2 %copy-start = (bf16[576,1152]{1,0:T(8,128)(2,1)S(1)}, bf16[576,1152]{1,0:T(8,128)(2,1)}, u32[]{:S(2)}) copy-start(bf16[576,1152]{1,0:T(8,128)(2,1)} %param.10) | copy-start | bytes 3981316
  7.2 67.0 %copy-start.9 = (bf16[1,128,576]{1,2,0:T(8,128)(2,1)S(1)}, bf16[1,128,576]{1,2,0:T(8,128)(2,1)}, u32[]{:S(2)}) copy-start(bf16[1,128,576]{1,2,0:T(8,128)(2,1)} %param.7) | copy-start | bytes 442372
  7.2 64.2 %all-gather.3.cloned.1.call-start = ((), (), s32[]{:S(2)}) async-start(), calls=%async_computation.3 | async-start | bytes 5013504 | tf_op jit(solution)/shard_map/all_gather | solution.py:36
  9.1 198.8 %all-gather.5.cloned.1.call-start = ((), (), s32[]{:S(2)}) async-start(), calls=%async_computation.4 | async-start | bytes 5013504 | tf_op jit(solution)/shard_map/all_gather | solution.py:36
  74.1 4.3 %copy-start.2 = (bf16[1,2048,576]{1,2,0:T(8,128)(2,1)}, bf16[1,2048,576]{1,2,0:T(8,128)(2,1)S(1)}, u32[]{:S(2)}) copy-start(bf16[1,2048,576]{1,2,0:T(8,128)(2,1)S(1)} %get-tuple-element.8) | copy-start | bytes 7077892
  74.1 4.3 %copy-start.5 = (bf16[1,2048,576]{1,2,0:T(8,128)(2,1)}, bf16[1,2048,576]{1,2,0:T(8,128)(2,1)S(1)}, u32[]{:S(2)}) copy-start(bf16[1,2048,576]{1,2,0:T(8,128)(2,1)S(1)} %get-tuple-element.7) | copy-start | bytes 7077892
  76.3 5.0 %copy-start.1 = (f32[8,2048,128]{2,1,0:T(8,128)}, f32[8,2048,128]{2,1,0:T(8,128)S(1)}, u32[]{:S(2)}) copy-start(f32[8,2048,128]{2,1,0:T(8,128)S(1)} %get-tuple-element.14) | copy-start | bytes 25165828
  78.4 3.0 %copy-start.11 = (bf16[1,128,1152]{2,1,0:T(8,128)(2,1)S(1)}, bf16[1,128,1152]{2,1,0:T(8,128)(2,1)}, u32[]{:S(2)}) copy-start(bf16[1,128,1152]{2,1,0:T(8,128)(2,1)} %param.11) | copy-start | bytes 884740
  81.4 3.8 %copy-start.7 = (bf16[128,8,72]{0,2,1:T(8,128)(2,1)}, bf16[128,8,72]{0,2,1:T(8,128)(2,1)S(1)}, u32[]{:S(2)}) copy-start(bf16[128,8,72]{0,2,1:T(8,128)(2,1)S(1)} %fusion.27) | copy-start | bytes 442372
  83.7 1.4 copy-start.8
  85.1 16.9 %all-to-all-start = ((f32[32,1,1]{2,1,0:T(1,128)}), f32[32,1,1]{2,1,0:T(1,128)S(1)}, u32[]{:S(2)}, u32[]{:S(2)}) async-start(f32[32,1,1]{2,1,0:T(1,128)} %broadcast_in_dim.100), calls=%async_computation | async-start | bytes 32768 | tf_op jit(solution)/shard_map/all_to_all | solution.py:23
  102.0 89.7 %all-to-all-start.1 = ((bf16[16,36,1152]{2,1,0:T(8,128)(2,1)}), bf16[16,36,1152]{2,1,0:T(8,128)(2,1)S(1)}, u32[]{:S(2)}, u32[]{:S(2)}) async-start(bf16[16,36,1152]{2,1,0:T(8,128)(2,1)} %reshape.133), calls=%async_computation.1 | async-start | bytes 2949120 | tf_op jit(solution)/shard_map/all_to_all | solution.py:53
  191.7 19.0 %copy-start.10 = (bf16[1,128,576]{1,2,0:T(8,128)(2,1)S(1)}, bf16[1,128,576]{1,2,0:T(8,128)(2,1)}, u32[]{:S(2)}) copy-start(bf16[1,128,576]{1,2,0:T(8,128)(2,1)} %param.8) | copy-start | bytes 442372
  193.9 12.9 %all-to-all-start.2 = ((bf16[32,2,648]{2,1,0:T(2,128)(2,1)}), bf16[32,2,648]{2,1,0:T(2,128)(2,1)S(1)}, u32[]{:S(2)}, u32[]{:S(2)}) async-start(bf16[32,2,648]{2,1,0:T(2,128)(2,1)} %reshape.136), calls=%async_computation.2 | async-start | bytes 196608 | tf_op jit(solution)/shard_map/all_to_all | solution.py:53
  207.9 4.3 %copy-start.12 = (pred[2048,128]{1,0:T(8,128)(4,1)S(1)}, pred[2048,128]{1,0:T(8,128)(4,1)}, u32[]{:S(2)}) copy-start(pred[2048,128]{1,0:T(8,128)(4,1)} %broadcast_compare_fusion) | copy-start | bytes 786436
  210.7 5.4 %copy-start.3 = (bf16[1,2048,576]{1,2,0:T(8,128)(2,1)}, bf16[1,2048,576]{1,2,0:T(8,128)(2,1)S(1)}, u32[]{:S(2)}) copy-start(bf16[1,2048,576]{1,2,0:T(8,128)(2,1)S(1)} %get-tuple-element.6) | copy-start | bytes 7077892
  210.7 5.4 %copy-start.6 = (bf16[1,2048,576]{1,2,0:T(8,128)(2,1)}, bf16[1,2048,576]{1,2,0:T(8,128)(2,1)S(1)}, u32[]{:S(2)}) copy-start(bf16[1,2048,576]{1,2,0:T(8,128)(2,1)S(1)} %get-tuple-element.5) | copy-start | bytes 7077892
  212.2 3.9 %copy-start.4 = (f32[8,2048,128]{2,1,0:T(8,128)}, f32[8,2048,128]{2,1,0:T(8,128)S(1)}, u32[]{:S(2)}) copy-start(f32[8,2048,128]{2,1,0:T(8,128)S(1)} %fusion.48) | copy-start | bytes 25165828
  212.2 3.9 %copy-start.13 = (bf16[1,128,576]{1,2,0:T(8,128)(2,1)S(1)}, bf16[1,128,576]{1,2,0:T(8,128)(2,1)}, u32[]{:S(2)}) copy-start(bf16[1,128,576]{1,2,0:T(8,128)(2,1)} %param.9) | copy-start | bytes 442372
Sparse Core Ops, SparseCore 0:
  10.6 60.7 all-gather.2
  84.6 78.2 all-gather.4
where the time goes:
time: 235 us; the launch traced here: 234 us
  blocking collectives  93.6 us (40%)
  waiting for transfers between devices  51 us (22%)
  matrix products  33.5 us (14%)
  starting transfers between devices  19 us (8%)
  between operations  18.1 us (8%)
  local copies, waits for them, and re-layouts  9.96 us (4%)
  other arithmetic  8.61 us (4%)
    psum x4, blocking collectives, by_axis(): value = lax.psum(value, axis)  55.2 us
    all_gather x2, waiting for transfers between devices, sent_together(): lax.all_gather(both, axis, axis=dim, tiled=True)  40.1 us
    all_gather x1, blocking collectives, local(): segment_all = lax.all_gather(segments, PATCH, axis=1, tiled=True)  21.1 us
    all_gather x1, blocking collectives, sent_together(): lax.all_gather(both, axis, axis=dim, tiled=True)  17.3 us
    all_to_all x2, starting transfers between devices, sum_at_owner(): lax.all_to_all(in_blocks(value, dim, peers), axis, 0, 0, tiled=True)  10.6 us
    dot_general x1, matrix products, query_grad_block(): jnp.einsum('hqk,khe->qhe', dscores, key_heads, preferred_element_type=jnp...  9.73 us
    dot_general x1, matrix products, key_grad_block(): jnp.einsum('hqk,qhe->khe', dscores, query_heads, preferred_element_type=j...  9.62 us
    all_to_all x1, starting transfers between devices, from_everyone(): return lax.all_to_all(copies, axis, split_axis=0, concat_axis=0, tiled=True)  8.3 us
  transfers between devices with their start and end apart: 5, of which 3 were waited for; matrix products, arithmetic and copies ran while one was open for 8% of the time, Pallas kernels for 0%

commit v1 on v0

v1 whole, which is shorter than its diff:
```python
import math

import jax
import jax.numpy as jnp
from jax import lax
from jax.experimental import pallas as pl
from jax.experimental.pallas import tpu as pltpu
from jax.sharding import Mesh
from jax.sharding import PartitionSpec as P

WIDTH = 1152
HEADS = 8
HD = 72
TOK = 128
FEAT = 576
SEQ = 2048
SAMPLES = 32
CHIPS = 8
PATCHES = 16
COLS = WIDTH // SAMPLES
ROWS = FEAT // PATCHES
PAD = 40
LANES = 640
BUF = 3 * HD + 8
QB = 256
NEG_LARGE = -1e30
SCALE = 1.0 / math.sqrt(HD)
EXP2_SCALE = SCALE * math.log2(math.e)
PATCH = ("patch_0", "patch_1")
DP = ("dp_0", "dp_1")
F32 = jnp.float32
BF16 = jnp.bfloat16

VM = pl.BlockSpec(memory_space=pltpu.VMEM)
SM = pl.BlockSpec(memory_space=pltpu.SMEM)


def call(kernel, name, out_shape, in_specs, flops, nbytes, scratch=(), out_specs=None):
    return pl.pallas_call(
        kernel,
        name=name,
        out_shape=out_shape,
        in_specs=in_specs,
        out_specs=out_specs if out_specs is not None else jax.tree.map(lambda _: VM, out_shape),
        scratch_shapes=list(scratch),
        cost_estimate=pl.CostEstimate(flops=flops, bytes_accessed=nbytes, transcendentals=0),
        compiler_params=pltpu.CompilerParams(vmem_limit_bytes=40 * 1024 * 1024),
    )


def dot(a, b, dims):
    return lax.dot_general(a, b, (dims, ((), ())), preferred_element_type=F32)


NN = ((1,), (0,))
NT = ((1,), (1,))


def pack_kernel(q_ref, k_ref, v_ref, seg_ref, out_ref):
    for at, ref in enumerate((q_ref, k_ref, v_ref)):
        for h in range(HEADS):
            out_ref[h, at * HD : (at + 1) * HD, :] = ref[0, h * HD : (h + 1) * HD, :]
    seg = jnp.broadcast_to(seg_ref[...].astype(F32), (8, TOK)).astype(BF16)
    for h in range(HEADS):
        out_ref[h, 3 * HD : BUF, :] = seg


def group_rows(ref, chip, core, length):
    seg = ref[chip, 3 * HD : BUF, :].astype(F32)[0:1]
    at = (2 * chip + core) * TOK + lax.broadcasted_iota(jnp.int32, (1, TOK), 1)
    return jnp.where(at < length, seg, -1.0)


def columns(ref, at):
    return jnp.concatenate([ref[c, at : at + HD, :] for c in range(CHIPS)], axis=1)


def forward_kernel(len_ref, own_ref, other_ref, attn_ref, probs_ref, inv_ref, key_sc, group_sc, value_sc):
    core = lax.axis_index("patch_1")
    length = len_ref[0]
    own_groups = []
    for side, ref in enumerate((own_ref, other_ref)):
        for c in range(CHIPS):
            at = (side * CHIPS + c) * TOK
            key_sc[at : at + TOK, :] = ref[c, HD : 2 * HD, :].astype(F32).T.astype(BF16)
            value_sc[:, at : at + TOK] = ref[c, 2 * HD : 3 * HD, :]
            group = group_rows(ref, c, core if side == 0 else 1 - core, length)
            if side == 0:
                own_groups.append(group)
            group_sc[at : at + TOK, :] = jnp.broadcast_to(group, (TOK, TOK)).T
    for b in range(SEQ // 2 // QB):
        pair = QB // TOK
        query = jnp.concatenate([own_ref[b * pair + i, 0:HD, :] for i in range(pair)], axis=1)
        group = jnp.concatenate([own_groups[b * pair + i] for i in range(pair)], axis=1)
        scores = dot(key_sc[...], query, NN)
        key_group = jnp.concatenate([group_sc[...]] * pair, axis=1)
        masked = jnp.where(key_group == group, scores, NEG_LARGE)
        top = jnp.max(masked, axis=0, keepdims=True)
        probs = jnp.exp2((masked - top) * EXP2_SCALE)
        inv = 1.0 / jnp.sum(probs, axis=0, keepdims=True)
        weights = probs.astype(BF16)
        probs_ref[b] = weights
        attn = (dot(value_sc[...], weights, NN) * inv).astype(BF16)
        inv_ref[b : b + 1, :] = inv
        for i in range(pair):
            attn_ref[b * pair + i] = attn[:, i * TOK : (i + 1) * TOK]


def project_kernel(len_ref, attn_ref, weight_ref, target_ref, back_ref, out_ref, loss_ref):
    place = 2 * lax.axis_index("patch_0") + lax.axis_index("patch_1")
    attn = attn_ref[...].reshape(FEAT, TOK).astype(F32).T.astype(BF16)
    output = dot(attn, weight_ref[...], NN)
    at = place * TOK + lax.broadcasted_iota(jnp.int32, (TOK, WIDTH), 0)
    error = jnp.where(at < len_ref[0], output - target_ref[0].astype(F32), 0.0)
    grad_out = (2.0 * error).astype(BF16)
    out_ref[...] = grad_out
    loss_ref[...] = jnp.sum(error * error, axis=0, keepdims=True)
    back = dot(weight_ref[...], grad_out, NT).astype(BF16)
    for h in range(HEADS):
        back_ref[h] = back[h * HD : (h + 1) * HD, :]


def high_low(value):
    high = value.astype(BF16).astype(F32)
    return high, value - high


def weight_kernel(len_ref, attn_ref, grad_ref, loss_ref, out_ref, acc):
    attn = attn_ref[...].reshape(FEAT, TOK)
    turned = grad_ref[...].astype(F32).T.astype(BF16)
    acc[...] = dot(turned, attn, NT)
    length = len_ref[0]
    upper = length // 256
    lower = length - upper * 256
    loss = jnp.broadcast_to(jnp.sum(loss_ref[...], axis=1, keepdims=True), (1, LANES))
    loss_high, loss_low = high_low(loss)
    rows = jnp.concatenate(
        [
            jnp.full((1, LANES), upper.astype(F32)),
            jnp.full((1, LANES), lower.astype(F32)),
            loss_high,
            loss_low,
        ],
        axis=0,
    )
    tail = jnp.zeros((PAD, LANES - FEAT), BF16)
    for d in range(SAMPLES):
        block = jnp.concatenate([acc[d * COLS : (d + 1) * COLS, :], rows[:, :FEAT]], axis=0)
        out_ref[d, :, 0:FEAT] = block.astype(BF16)
        out_ref[d, :, FEAT:LANES] = tail


def backward_kernel(own_ref, other_ref, attn_ref, back_ref, probs_ref, inv_ref, query_out, own_out, other_out, value_sc, key_sc, key_acc, value_acc):
    for side, ref in enumerate((own_ref, other_ref)):
        for c in range(CHIPS):
            at = (side * CHIPS + c) * TOK
            value_sc[at : at + TOK, :] = ref[c, 2 * HD : 3 * HD, :].astype(F32).T.astype(BF16)
            key_sc[:, at : at + TOK] = ref[c, HD : 2 * HD, :]
    for b in range(SEQ // 2 // QB):
        pair = QB // TOK
        chips = range(b * pair, (b + 1) * pair)
        query = jnp.concatenate([own_ref[c, 0:HD, :] for c in chips], axis=1)
        attn = jnp.concatenate([attn_ref[c] for c in chips], axis=1)
        back = jnp.concatenate([back_ref[c] for c in chips], axis=1)
        back = (back.astype(F32) * inv_ref[b : b + 1, :]).astype(BF16)
        delta = jnp.sum(back.astype(F32) * attn.astype(F32), axis=0, keepdims=True)
        probs = probs_ref[b]
        dprobs = dot(value_sc[...], back, NN)
        dscores = (probs.astype(F32) * (dprobs - delta)).astype(BF16)
        query_grad = dot(key_sc[...], dscores, NN).astype(BF16)
        for i, c in enumerate(chips):
            query_out[c] = query_grad[:, i * TOK : (i + 1) * TOK]
        key_part = dot(query, dscores, NT)
        value_part = dot(back, probs, NT)
        if b == 0:
            key_acc[...] = key_part
            value_acc[...] = value_part
        else:
            key_acc[...] += key_part
            value_acc[...] += value_part
    for side, ref in enumerate((own_out, other_out)):
        for c in range(CHIPS):
            at = (side * CHIPS + c) * TOK
            ref[c, 0:HD, :] = key_acc[:, at : at + TOK].astype(BF16)
            ref[c, HD : 2 * HD, :] = value_acc[:, at : at + TOK].astype(BF16)


def join_kernel(query_ref, own_ref, other_ref, out_ref):
    out_ref[:, 0:HD, :] = query_ref[...]
    out_ref[:, HD : 3 * HD, :] = (own_ref[...].astype(F32) + other_ref[...].astype(F32)).astype(BF16)


def reduce_kernel(part_ref, out_ref, stat_ref):
    total = part_ref[0].astype(F32)
    for d in range(1, SAMPLES):
        total = total + part_ref[d].astype(F32)
    count = 256.0 * total[COLS : COLS + 1, 0:TOK] + total[COLS + 1 : COLS + 2, 0:TOK]
    loss = total[COLS + 2 : COLS + 3, 0:TOK] + total[COLS + 3 : COLS + 4, 0:TOK]
    stat_ref[...] = jnp.broadcast_to(count, (8, TOK))
    loss_high, loss_low = high_low(loss)
    turned = jnp.concatenate([total, jnp.zeros((TOK - PAD, LANES), F32)], axis=0).T
    tail = jnp.concatenate([loss_high, loss_low, jnp.zeros((PAD - ROWS - 2, TOK), F32)], axis=0)
    for p in range(PATCHES):
        out_ref[p] = jnp.concatenate([turned[p * ROWS : (p + 1) * ROWS, :], tail], axis=0).astype(BF16)


def unpack_kernel(rows_ref, stat_ref, query_ref, key_ref, value_ref):
    ratio = float(SAMPLES * SEQ) / stat_ref[0:1, :]
    for at, (ref, factor) in enumerate(((query_ref, SCALE), (key_ref, SCALE), (value_ref, 1.0))):
        for h in range(HEADS):
            rows = rows_ref[h, at * HD : (at + 1) * HD, :].astype(F32)
            ref[0, h * HD : (h + 1) * HD, :] = rows * (ratio * factor)


def last_kernel(part_ref, stat_ref, weight_ref, loss_ref):
    total = part_ref[0].astype(F32)
    for p in range(1, PATCHES):
        total = total + part_ref[p].astype(F32)
    count = stat_ref[0:1, :]
    ratio = float(SAMPLES * SEQ) / count
    weight_ref[...] = (total[0:ROWS, :] * (ratio / SEQ))[:, 0:COLS]
    loss_ref[...] = (total[ROWS : ROWS + 1, :] + total[ROWS + 1 : ROWS + 2, :]) / (count * WIDTH)


def exchange(value, axis):
    return lax.all_to_all(value, axis, 0, 0, tiled=True)


def swap(value):
    return lax.ppermute(value, "patch_1", [(0, 1), (1, 0)])


def shape(dims, dtype):
    return jax.ShapeDtypeStruct(dims, dtype)


def local(query_rows, key_rows, value_rows, out_weight, target, lengths, segments):
    buffer = shape((CHIPS, BUF, TOK), BF16)
    heads = shape((CHIPS, HD, TOK), BF16)
    packed = call(pack_kernel, "pack", buffer, [VM] * 4, 10**6, 10**6)(
        *(jnp.swapaxes(rows, 1, 2) for rows in (query_rows, key_rows, value_rows)), segments
    )
    own = exchange(packed, "patch_0")
    other = swap(own)
    blocks = SEQ // 2 // QB
    attn, probs, inv = call(
        forward_kernel,
        "forward",
        (heads, shape((blocks, SEQ, QB), BF16), shape((blocks, QB), F32)),
        [SM, VM, VM],
        4 * HD * SEQ * SEQ // 2,
        6 * 10**6,
        [pltpu.VMEM((SEQ, HD), BF16), pltpu.VMEM((SEQ, TOK), F32), pltpu.VMEM((HD, SEQ), BF16)],
    )(lengths, own, other)
    attn_rows = exchange(attn, "patch_0")
    back, grad_out, loss_part = call(
        project_kernel,
        "project",
        (heads, shape((TOK, WIDTH), BF16), shape((1, WIDTH), F32)),
        [SM, VM, VM, VM],
        4 * TOK * FEAT * WIDTH,
        3 * 10**6,
    )(lengths, attn_rows, out_weight, target)
    back_heads = exchange(back, "patch_0")
    weight_part = call(
        weight_kernel,
        "weight",
        shape((SAMPLES, PAD, LANES), BF16),
        [SM, VM, VM, VM],
        2 * TOK * FEAT * WIDTH,
        3 * 10**6,
        [pltpu.VMEM((WIDTH, FEAT), F32)],
    )(lengths, attn_rows, grad_out, loss_part)
    weight_parts = exchange(weight_part, DP)
    pair = shape((CHIPS, 2 * HD, TOK), BF16)
    query_grad, own_grad, other_grad = call(
        backward_kernel,
        "backward",
        (heads, pair, pair),
        [VM] * 6,
        8 * HD * SEQ * SEQ // 2,
        6 * 10**6,
        [
            pltpu.VMEM((SEQ, HD), BF16),
            pltpu.VMEM((HD, SEQ), BF16),
            pltpu.VMEM((HD, SEQ), F32),
            pltpu.VMEM((HD, SEQ), F32),
        ],
    )(own, other, attn, back_heads, probs, inv)
    got = swap(other_grad)
    joined = call(join_kernel, "join", shape((CHIPS, 3 * HD, TOK), BF16), [VM] * 3, 10**6, 10**6)(
        query_grad, own_grad, got
    )
    grads = exchange(joined, "patch_0")
    reduced, stats = call(
        reduce_kernel,
        "reduce",
        (shape((PATCHES, PAD, TOK), BF16), shape((8, TOK), F32)),
        [VM],
        10**6,
        2 * 10**6,
    )(weight_parts)
    weight_last = exchange(reduced, PATCH)
    rows = shape((1, FEAT, TOK), F32)
    query_out, key_out, value_out = call(
        unpack_kernel, "unpack", (rows, rows, rows), [VM, VM], 10**6, 10**6
    )(grads, stats)
    weight_grad, loss = call(
        last_kernel, "last", (shape((ROWS, COLS), F32), shape((1, TOK), F32)), [VM, VM], 10**5, 10**5
    )(weight_last, stats)
    grads_out = (jnp.swapaxes(rows, 1, 2) for rows in (query_out, key_out, value_out))
    return *grads_out, weight_grad, loss[0, 0]


def solution(mesh):
    torus = Mesh(mesh.devices.reshape(4, 8, 8, 2), ("dp_0", "dp_1", "patch_0", "patch_1"))
    return jax.shard_map(
        local,
        mesh=torus,
        in_specs=(
            P(DP, PATCH, None),
            P(DP, PATCH, None),
            P(DP, PATCH, None),
            P(),
            P(DP, PATCH, None),
            P(DP),
            P(DP, PATCH),
        ),
        out_specs=(P(DP, PATCH, None), P(DP, PATCH, None), P(DP, PATCH, None), P(PATCH, DP), P()),
        check_vma=False,
    )
```

time: 235 us -> 150 us (0.64)
  blocking collectives: 93.6 us -> 32.7 us
  matrix products: 33.5 us -> 0 us
  starting transfers between devices: 19 us -> 38.8 us
  Pallas kernels: 0 us -> 17.6 us
  between operations: 18.1 us -> 1.39 us
  other arithmetic: 8.61 us -> 0 us
  local copies, waits for them, and re-layouts: 9.96 us -> 7.5 us
    psum x4 -> x0, blocking collectives: 55.2 us -> none  [by_axis(): value = lax.psum(value, axis)]
    all_gather x2 -> x0, waiting for transfers between devices: 40.1 us -> none  [sent_together(): lax.all_gather(both, axis, axis=dim, tiled=True)]
    all_gather x2 -> x0, blocking collectives: 38.4 us -> none  [the longest x1 21.1 us: local(): segment_all = lax.all_gather(segments, PATCH, axis=1, tiled=True)]
    all_to_all x3 -> x4, waiting for transfers between devices: 10.9 us -> 48.8 us  [exchange(): return lax.all_to_all(value, axis, 0, 0, tiled=True)]
    dot_general x9 -> x0, matrix products: 33.5 us -> none  [the longest x1 9.73 us: query_grad_block(): jnp.einsum('hqk,khe->qhe', dscores, key_heads, preferred_element_type=jnp...]
    all_to_all x0 -> x2, blocking collectives: none -> 32.7 us  [exchange(): return lax.all_to_all(value, axis, 0, 0, tiled=True)]
    pallas_call x0 -> x9, Pallas kernels: none -> 17.6 us  [the longest x1 5.97 us: local(): call(forward_kernel, 'forward', (heads, shape((blocks, SEQ, QB), BF16), s...]
    all_to_all x3 -> x4, starting transfers between devices: 18.9 us -> 29 us  [exchange(): return lax.all_to_all(value, axis, 0, 0, tiled=True)]
  transfers between devices with their start and end apart: 5 -> 6, of which waited for: 3 -> 6; matrix products, arithmetic and copies ran while one was open for 8% -> 0% of each run, Pallas kernels for 0% -> 6%
where the time goes in v1:
time: 150 us; the launch traced here: 149 us
  waiting for transfers between devices  50.8 us (34%)
  starting transfers between devices  38.8 us (26%)
  blocking collectives  32.7 us (22%)
  Pallas kernels  17.6 us (12%)
  local copies, waits for them, and re-layouts  7.5 us (5%)
    all_to_all x4, waiting for transfers between devices, exchange(): return lax.all_to_all(value, axis, 0, 0, tiled=True)  48.8 us
    all_to_all x2, blocking collectives, exchange(): return lax.all_to_all(value, axis, 0, 0, tiled=True)  32.7 us
    all_to_all x4, starting transfers between devices, exchange(): return lax.all_to_all(value, axis, 0, 0, tiled=True)  29 us
    ppermute x2, starting transfers between devices, swap(): return lax.ppermute(value, 'patch_1', [(0, 1), (1, 0)])  9.84 us
    unnamed x16, local copies, waits for them, and re-layouts  7.5 us
    pallas_call x1, Pallas kernels, local(): call(forward_kernel, 'forward', (heads, shape((blocks, SEQ, QB), BF16), s...  5.97 us
    pallas_call x1, Pallas kernels, local(): call(backward_kernel, 'backward', (heads, pair, pair), [VM] * 6, 8 * HD *...  4.68 us
  transfers between devices with their start and end apart: 6, of which 6 were waited for; matrix products, arithmetic and copies ran while one was open for 0% of the time, Pallas kernels for 6%

profile of v1, /device:TPU:1, one launch (start us, length us, event | category | flops | bytes accessed | tf_op | source)
XLA Modules:
  0.0 148.8 jit_solution(15981179580505780888)
XLA Ops:
  0.6 0.0 copy-start.4
  0.6 0.9 copy-done.4
  1.5 0.9 copy-done.5
  2.5 0.9 copy-done.6
  3.4 0.7 copy-done.7
  4.1 0.0 copy-start.2
  4.1 0.0 copy-start.3
  4.1 21.7 %all_to_all.30.own_ref = bf16[8,224,128]{2,1,0:T(8,128)(2,1)S(1)} all-to-all(bf16[8,224,128]{2,1,0:T(8,128)(2,1)S(1)} %pack.1), channel_id=1, replica_groups=mesh['dp_0'=4,'dp_1'=8,'patch_0'=8,'patch_1'=2] {'patch_0'}, dimensions={0} | all-to-all | bytes 917504 | tf_op jit(solution)/shard_map/all_to_all | solution.py:226
  25.7 4.9 %collective-permute-start = (bf16[8,224,128]{2,1,0:T(8,128)(2,1)S(1)}, bf16[8,224,128]{2,1,0:T(8,128)(2,1)S(1)}, u32[]{:S(2)}, u32[]{:S(2)}) collective-permute-start(bf16[8,224,128]{2,1,0:T(8,128)(2,1)S(1)} %all_to_all.30.own_ref), channel_id=1, source_target_pairs={{0,1},{1,0},{2,3},{3,2},{4,5},{5,4},{6,7},{7,6},{8,9},{9,8},{10,11... | collective-permute-start | bytes 1376264 | tf_op jit(solution)/shard_map/ppermute | solution.py:230
  31.2 0.8 collective-permute-done.other_ref
  32.0 6.0 %forward.1 = (bf16[8,72,128]{2,1,0:T(8,128)(2,1)S(1)}, bf16[4,2048,256]{2,1,0:T(8,128)(2,1)S(1)}, f32[4,256]{1,0:T(4,128)S(1)}) custom-call(s32[1]{0:T(128)S(6)} %copy.12.len_ref, bf16[8,224,128]{2,1,0:T(8,128)(2,1)S(1)} %all_to_all.30.own_ref, bf16[8,224,128]{2,1,0:T(8,128)(2,1)S(1)} %collective-permute-done.other_ref), custom_call_target="tpu_custom_call" | custom-call | flops 603979776 | bytes 6000000 | tf_op jit(solution)/shard_map/forward/pallas_call | solution.py:246
  38.0 1.9 %copy-done = bf16[4,2048,256]{2,1,0:T(8,128)(2,1)} copy-done((bf16[4,2048,256]{2,1,0:T(8,128)(2,1)}, bf16[4,2048,256]{2,1,0:T(8,128)(2,1)S(1)}, u32[]{:S(2)}) %copy-start) | copy-done | bytes 4194328
  39.9 11.1 %all_to_all.31.attn_ref = bf16[8,72,128]{2,1,0:T(8,128)(2,1)S(1)} all-to-all(bf16[8,72,128]{2,1,0:T(8,128)(2,1)S(1)} %get-tuple-element.21.attn_ref), channel_id=1, replica_groups=mesh['dp_0'=4,'dp_1'=8,'patch_0'=8,'patch_1'=2] {'patch_0'}, dimensions={0} | all-to-all | bytes 294912 | tf_op jit(solution)/shard_map/all_to_all | solution.py:226
  51.0 1.6 %project.1 = (bf16[8,72,128]{2,1,0:T(8,128)(2,1)}, bf16[128,1152]{1,0:T(8,128)(2,1)S(1)}, f32[1,1152]{1,0:T(1,128)S(1)}) custom-call(s32[1]{0:T(128)S(6)} %copy.12.len_ref, bf16[8,72,128]{2,1,0:T(8,128)(2,1)S(1)} %all_to_all.31.attn_ref, bf16[576,1152]{1,0:T(8,128)(2,1)S(1)} %copy-done.2, bf16[1,128,1152]{2,1,0:T(8,128)(2,1)S(1)} %copy-done.3), custom_call_target="tpu_custom_call" | custom-call | flops 339738624 | bytes 3000000 | tf_op jit(solution)/shard_map/project/pallas_call | solution.py:256
  52.6 3.4 %all-to-all-start.2 = ((bf16[8,72,128]{2,1,0:T(8,128)(2,1)}), bf16[8,72,128]{2,1,0:T(8,128)(2,1)S(1)}, u32[]{:S(2)}, u32[]{:S(2)}) async-start(bf16[8,72,128]{2,1,0:T(8,128)(2,1)} %get-tuple-element.22), calls=%async_computation.2 | async-start | bytes 294912 | tf_op jit(solution)/shard_map/all_to_all | solution.py:226
  56.0 1.9 %weight.1 = bf16[32,40,640]{2,1,0:T(8,128)(2,1)} custom-call(s32[1]{0:T(128)S(6)} %copy.12.len_ref, bf16[8,72,128]{2,1,0:T(8,128)(2,1)S(1)} %all_to_all.31.attn_ref, bf16[128,1152]{1,0:T(8,128)(2,1)S(1)} %get-tuple-element.28.grad_ref, f32[1,1152]{1,0:T(1,128)S(1)} %get-tuple-element.29.loss_ref), custom_call_target="tpu_custom_call" | custom-call | flops 169869312 | bytes 3000000 | tf_op jit(solution)/shard_map/weight/pallas_call | solution.py:265
  57.9 6.1 %all-to-all-done.2.back_ref = bf16[8,72,128]{2,1,0:T(8,128)(2,1)S(1)} async-done(((bf16[8,72,128]{2,1,0:T(8,128)(2,1)}), bf16[8,72,128]{2,1,0:T(8,128)(2,1)S(1)}, u32[]{:S(2)}, u32[]{:S(2)}) %all-to-all-start.2) | async-done | bytes 147488 | tf_op jit(solution)/shard_map/all_to_all | solution.py:226
  64.0 12.9 %all-to-all-start.4 = ((bf16[32,40,640]{2,1,0:T(8,128)(2,1)}), bf16[32,40,640]{2,1,0:T(8,128)(2,1)S(1)}, u32[]{:S(2)}, u32[]{:S(2)}) async-start(bf16[32,40,640]{2,1,0:T(8,128)(2,1)} %weight.1), calls=%async_computation.4 | async-start | bytes 3276800 | tf_op jit(solution)/shard_map/all_to_all | solution.py:226
  76.9 0.0 copy-start.1
  76.9 2.2 %copy-done.1 = bf16[4,2048,256]{2,1,0:T(8,128)(2,1)S(1)} copy-done((bf16[4,2048,256]{2,1,0:T(8,128)(2,1)S(1)}, bf16[4,2048,256]{2,1,0:T(8,128)(2,1)}, u32[]{:S(2)}) %copy-start.1) | copy-done | bytes 4194328
  79.1 4.7 %backward.1 = (bf16[8,72,128]{2,1,0:T(8,128)(2,1)S(1)}, bf16[8,144,128]{2,1,0:T(8,128)(2,1)S(1)}, bf16[8,144,128]{2,1,0:T(8,128)(2,1)S(1)}) custom-call(bf16[8,224,128]{2,1,0:T(8,128)(2,1)S(1)} %all_to_all.30.own_ref, bf16[8,224,128]{2,1,0:T(8,128)(2,1)S(1)} %collective-permute-done.other_ref, bf16[8,72,128]{2,1,0:T(8,128)(2,1)S(1)} %get-tuple-element.21.attn_ref, ...), custom_call_target="tpu_custom_call" | custom-call | flops 1207959552 | bytes 6000000 | tf_op jit(solution)/shard_map/backward/pallas_call | solution.py:276
  83.8 5.0 %collective-permute-start.1 = (bf16[8,144,128]{2,1,0:T(8,128)(2,1)S(1)}, bf16[8,144,128]{2,1,0:T(8,128)(2,1)S(1)}, u32[]{:S(2)}, u32[]{:S(2)}) collective-permute-start(bf16[8,144,128]{2,1,0:T(8,128)(2,1)S(1)} %get-tuple-element.27), channel_id=1, source_target_pairs={{0,1},{1,0},{2,3},{3,2},{4,5},{5,4},{6,7},{7,6},{8,9},{9,8},{10,11... | collective-permute-start | bytes 884744 | tf_op jit(solution)/shard_map/ppermute | solution.py:230
  88.8 1.2 collective-permute-done.1.other_ref
  90.0 0.8 join.1
  90.8 24.2 %all-to-all-done.4.part_ref = bf16[32,40,640]{2,1,0:T(8,128)(2,1)S(1)} async-done(((bf16[32,40,640]{2,1,0:T(8,128)(2,1)}), bf16[32,40,640]{2,1,0:T(8,128)(2,1)S(1)}, u32[]{:S(2)}, u32[]{:S(2)}) %all-to-all-start.4) | async-done | bytes 1638432 | tf_op jit(solution)/shard_map/all_to_all | solution.py:226
  115.1 3.5 %all-to-all-start.3 = ((bf16[8,216,128]{2,1,0:T(8,128)(2,1)}), bf16[8,216,128]{2,1,0:T(8,128)(2,1)S(1)}, u32[]{:S(2)}, u32[]{:S(2)}) async-start(bf16[8,216,128]{2,1,0:T(8,128)(2,1)} %join.1), calls=%async_computation.3 | async-start | bytes 884736 | tf_op jit(solution)/shard_map/all_to_all | solution.py:226
  118.5 1.0 reduce.1
  119.5 9.8 %all-to-all-done.3.rows_ref = bf16[8,216,128]{2,1,0:T(8,128)(2,1)S(1)} async-done(((bf16[8,216,128]{2,1,0:T(8,128)(2,1)}), bf16[8,216,128]{2,1,0:T(8,128)(2,1)S(1)}, u32[]{:S(2)}, u32[]{:S(2)}) %all-to-all-start.3) | async-done | bytes 442400 | tf_op jit(solution)/shard_map/all_to_all | solution.py:226
  129.3 9.3 %all-to-all-start.5 = ((bf16[16,40,128]{2,1,0:T(8,128)(2,1)}), bf16[16,40,128]{2,1,0:T(8,128)(2,1)S(1)}, u32[]{:S(2)}, u32[]{:S(2)}) async-start(bf16[16,40,128]{2,1,0:T(8,128)(2,1)} %get-tuple-element.34), calls=%async_computation.5 | async-start | bytes 327680 | tf_op jit(solution)/shard_map/all_to_all | solution.py:226
  138.5 0.9 unpack.1
  139.5 8.7 %all-to-all-done.5.part_ref = bf16[16,40,128]{2,1,0:T(8,128)(2,1)S(1)} async-done(((bf16[16,40,128]{2,1,0:T(8,128)(2,1)}), bf16[16,40,128]{2,1,0:T(8,128)(2,1)S(1)}, u32[]{:S(2)}, u32[]{:S(2)}) %all-to-all-start.5) | async-done | bytes 163872 | tf_op jit(solution)/shard_map/all_to_all | solution.py:226
  148.2 0.6 last.1
  (7 shorter events, 0.0 us)
Async XLA Ops:
  0.6 0.9 copy-start.4
  1.5 0.9 copy-start.5
  2.5 0.9 copy-start.6
  3.4 0.7 copy-start.7
  4.1 47.0 %copy-start.2 = (bf16[576,1152]{1,0:T(8,128)(2,1)S(1)}, bf16[576,1152]{1,0:T(8,128)(2,1)}, u32[]{:S(2)}) copy-start(bf16[576,1152]{1,0:T(8,128)(2,1)} %weight_ref.1) | copy-start | bytes 3981316
  4.1 46.9 %copy-start.3 = (bf16[1,128,1152]{2,1,0:T(8,128)(2,1)S(1)}, bf16[1,128,1152]{2,1,0:T(8,128)(2,1)}, u32[]{:S(2)}) copy-start(bf16[1,128,1152]{2,1,0:T(8,128)(2,1)} %target_ref.1) | copy-start | bytes 884740
  25.7 6.3 %collective-permute-start = (bf16[8,224,128]{2,1,0:T(8,128)(2,1)S(1)}, bf16[8,224,128]{2,1,0:T(8,128)(2,1)S(1)}, u32[]{:S(2)}, u32[]{:S(2)}) collective-permute-start(bf16[8,224,128]{2,1,0:T(8,128)(2,1)S(1)} %all_to_all.30.own_ref), channel_id=1, source_target_pairs={{0,1},{1,0},{2,3},{3,2},{4,5},{5,4},{6,7},{7,6},{8,9},{9,8},{10,11... | collective-permute-start | bytes 1376264 | tf_op jit(solution)/shard_map/ppermute | solution.py:230
  38.0 1.9 %copy-start = (bf16[4,2048,256]{2,1,0:T(8,128)(2,1)}, bf16[4,2048,256]{2,1,0:T(8,128)(2,1)S(1)}, u32[]{:S(2)}) copy-start(bf16[4,2048,256]{2,1,0:T(8,128)(2,1)S(1)} %get-tuple-element.23.probs_ref) | copy-start | bytes 12582916
  52.6 11.4 %all-to-all-start.2 = ((bf16[8,72,128]{2,1,0:T(8,128)(2,1)}), bf16[8,72,128]{2,1,0:T(8,128)(2,1)S(1)}, u32[]{:S(2)}, u32[]{:S(2)}) async-start(bf16[8,72,128]{2,1,0:T(8,128)(2,1)} %get-tuple-element.22), calls=%async_computation.2 | async-start | bytes 294912 | tf_op jit(solution)/shard_map/all_to_all | solution.py:226
  64.0 51.0 %all-to-all-start.4 = ((bf16[32,40,640]{2,1,0:T(8,128)(2,1)}), bf16[32,40,640]{2,1,0:T(8,128)(2,1)S(1)}, u32[]{:S(2)}, u32[]{:S(2)}) async-start(bf16[32,40,640]{2,1,0:T(8,128)(2,1)} %weight.1), calls=%async_computation.4 | async-start | bytes 3276800 | tf_op jit(solution)/shard_map/all_to_all | solution.py:226
  76.9 2.2 %copy-start.1 = (bf16[4,2048,256]{2,1,0:T(8,128)(2,1)S(1)}, bf16[4,2048,256]{2,1,0:T(8,128)(2,1)}, u32[]{:S(2)}) copy-start(bf16[4,2048,256]{2,1,0:T(8,128)(2,1)} %copy-done) | copy-start | bytes 12582916
  83.8 6.2 %collective-permute-start.1 = (bf16[8,144,128]{2,1,0:T(8,128)(2,1)S(1)}, bf16[8,144,128]{2,1,0:T(8,128)(2,1)S(1)}, u32[]{:S(2)}, u32[]{:S(2)}) collective-permute-start(bf16[8,144,128]{2,1,0:T(8,128)(2,1)S(1)} %get-tuple-element.27), channel_id=1, source_target_pairs={{0,1},{1,0},{2,3},{3,2},{4,5},{5,4},{6,7},{7,6},{8,9},{9,8},{10,11... | collective-permute-start | bytes 884744 | tf_op jit(solution)/shard_map/ppermute | solution.py:230
  115.1 14.2 %all-to-all-start.3 = ((bf16[8,216,128]{2,1,0:T(8,128)(2,1)}), bf16[8,216,128]{2,1,0:T(8,128)(2,1)S(1)}, u32[]{:S(2)}, u32[]{:S(2)}) async-start(bf16[8,216,128]{2,1,0:T(8,128)(2,1)} %join.1), calls=%async_computation.3 | async-start | bytes 884736 | tf_op jit(solution)/shard_map/all_to_all | solution.py:226
  129.3 18.9 %all-to-all-start.5 = ((bf16[16,40,128]{2,1,0:T(8,128)(2,1)}), bf16[16,40,128]{2,1,0:T(8,128)(2,1)S(1)}, u32[]{:S(2)}, u32[]{:S(2)}) async-start(bf16[16,40,128]{2,1,0:T(8,128)(2,1)} %get-tuple-element.34), calls=%async_computation.5 | async-start | bytes 327680 | tf_op jit(solution)/shard_map/all_to_all | solution.py:226

commit v2 on v1

v2 whole, which is shorter than its diff:
```python
import math

import jax
import jax.numpy as jnp
from jax import lax
from jax.experimental import pallas as pl
from jax.experimental.pallas import tpu as pltpu
from jax.sharding import Mesh
from jax.sharding import PartitionSpec as P


WIDTH = 1152
HEADS = 8
HD = 72
TOK = 128
FEAT = 576
SEQ = 2048
SAMPLES = 32
CHIPS = 8
PATCHES = 16
COLS = WIDTH // SAMPLES
ROWS = FEAT // PATCHES
HALF = FEAT // 2
STAT = COLS * HALF // TOK
PAD = 88
LAST = ROWS + 4
PAIR = WIDTH + HALF + 8
BUF = 3 * HD + 8
QB = 256
NEG_LARGE = -1e30
SCALE = 1.0 / math.sqrt(HD)
EXP2_SCALE = SCALE * math.log2(math.e)
PATCH = ("patch_0", "patch_1")
DP = ("dp_0", "dp_1")
F32 = jnp.float32
BF16 = jnp.bfloat16

VM = pl.BlockSpec(memory_space=pltpu.VMEM)
SM = pl.BlockSpec(memory_space=pltpu.SMEM)
HB = pl.BlockSpec(memory_space=pltpu.HBM)
ANY = pl.BlockSpec(memory_space=pl.ANY)


def call(kernel, out_shape, in_specs, flops, nbytes, scratch=(), limit=16, outs=None, aliases=None):
    return pl.pallas_call(
        kernel,
        out_shape=out_shape,
        in_specs=in_specs,
        out_specs=outs if outs is not None else jax.tree.map(lambda _: VM, out_shape),
        scratch_shapes=list(scratch),
        input_output_aliases=aliases or {},
        cost_estimate=pl.CostEstimate(flops=flops, bytes_accessed=nbytes, transcendentals=0),
        compiler_params=pltpu.CompilerParams(vmem_limit_bytes=limit * 1024 * 1024),
    )


def dot(a, b, dims):
    return lax.dot_general(a, b, (dims, ((), ())), preferred_element_type=F32)


NN = ((1,), (0,))
NT = ((1,), (1,))


def pack_kernel(q_ref, k_ref, v_ref, seg_ref, out_ref, seg_sc, sems):
    copies = [
        pltpu.make_async_copy(ref, out_ref.at[:, at * HD : (at + 1) * HD, :], sems.at[at])
        for at, ref in enumerate((q_ref, k_ref, v_ref))
    ]
    copies.append(pltpu.make_async_copy(seg_ref, seg_sc, sems.at[3]))
    for copy in copies:
        copy.start()
    copies[3].wait()
    seg = jnp.broadcast_to(seg_sc[...].astype(F32), (8, TOK)).astype(BF16)
    for h in range(HEADS):
        out_ref[h, 3 * HD : BUF, :] = seg
    for copy in copies[:3]:
        copy.wait()


def group_rows(ref, chip, core, length):
    seg = ref[chip, 3 * HD : BUF, :].astype(F32)[0:1]
    at = (2 * chip + core) * TOK + lax.broadcasted_iota(jnp.int32, (1, TOK), 1)
    return jnp.where(at < length, seg, -1.0)


def forward_kernel(
    len_ref, own_ref, other_ref, attn_ref, probs_ref, inv_ref, key_sc, group_sc, value_sc, probs_sc, sems
):
    core = lax.axis_index("patch_1")
    length = len_ref[0]
    own_groups = []
    copies = []
    for side, ref in enumerate((own_ref, other_ref)):
        for c in range(CHIPS):
            at = (side * CHIPS + c) * TOK
            key_sc[at : at + TOK, :] = ref[c, HD : 2 * HD, :].astype(F32).T.astype(BF16)
            value_sc[:, at : at + TOK] = ref[c, 2 * HD : 3 * HD, :]
            group = group_rows(ref, c, core if side == 0 else 1 - core, length)
            if side == 0:
                own_groups.append(group)
            group_sc[at : at + TOK, :] = jnp.broadcast_to(group, (TOK, TOK)).T
    for b in range(SEQ // 2 // QB):
        pair = QB // TOK
        query = jnp.concatenate([own_ref[b * pair + i, 0:HD, :] for i in range(pair)], axis=1)
        group = jnp.concatenate([own_groups[b * pair + i] for i in range(pair)], axis=1)
        scores = dot(key_sc[...], query, NN)
        key_group = jnp.concatenate([group_sc[...]] * pair, axis=1)
        masked = jnp.where(key_group == group, scores, NEG_LARGE)
        top = jnp.max(masked, axis=0, keepdims=True)
        probs = jnp.exp2((masked - top) * EXP2_SCALE)
        inv = 1.0 / jnp.sum(probs, axis=0, keepdims=True)
        weights = probs.astype(BF16)
        probs_sc[b] = weights
        copies.append(pltpu.make_async_copy(probs_sc.at[b], probs_ref.at[b], sems.at[b]))
        copies[b].start()
        attn = (dot(value_sc[...], weights, NN) * inv).astype(BF16)
        inv_ref[b : b + 1, :] = inv
        for i in range(pair):
            attn_ref[b * pair + i] = attn[:, i * TOK : (i + 1) * TOK]
    for copy in copies:
        copy.wait()


def high_low(value):
    high = value.astype(BF16).astype(F32)
    return high, value - high


def project_kernel(len_ref, attn_ref, weight_ref, target_ref, back_ref, out_ref, loss_ref):
    place = 2 * lax.axis_index("patch_0") + lax.axis_index("patch_1")
    attn = attn_ref[...].reshape(FEAT, TOK).astype(F32).T.astype(BF16)
    output = dot(attn, weight_ref[...], NN)
    at = place * TOK + lax.broadcasted_iota(jnp.int32, (TOK, WIDTH), 0)
    error = jnp.where(at < len_ref[0], output - target_ref[0].astype(F32), 0.0)
    grad_out = (2.0 * error).T.astype(BF16)
    back = dot(weight_ref[...], grad_out, NN).astype(BF16)
    for h in range(HEADS):
        back_ref[h] = back[h * HD : (h + 1) * HD, :]
    out_ref[...] = grad_out
    loss = jnp.sum(error * error, axis=0, keepdims=True)
    loss_ref[...] = sum(loss[:, i * TOK : (i + 1) * TOK] for i in range(WIDTH // TOK))


def pair_kernel(attn_ref, grad_ref, loss_ref, pair_ref, half_ref):
    first = lax.axis_index("patch_1") == 0
    wide = attn_ref[...].reshape(FEAT, TOK).astype(F32)
    sides = []
    for side in (0, 1):
        pieces = [wide[p * ROWS : (p + 1) * ROWS] for p in range(side, PATCHES, 2)]
        sides.append(jnp.concatenate(pieces, axis=0))
    half_ref[...] = jnp.where(first, sides[0], sides[1]).astype(BF16)
    stats = jnp.concatenate([*high_low(loss_ref[...]), jnp.zeros((6, TOK), F32)], axis=0)
    pair_ref[0:WIDTH, :] = grad_ref[...]
    pair_ref[WIDTH : WIDTH + HALF, :] = jnp.where(first, sides[1], sides[0]).astype(BF16)
    pair_ref[WIDTH + HALF : PAIR, :] = stats.astype(BF16)


def weight_kernel(len_ref, mine_ref, got_ref, half_ref, out_ref, acc):
    left = jnp.concatenate([mine_ref[0:WIDTH, :], got_ref[0:WIDTH, :]], axis=1)
    right = jnp.concatenate([half_ref[...], got_ref[WIDTH : WIDTH + HALF, :]], axis=1)
    acc[:, 0:HALF] = dot(left, right, NT)
    upper = len_ref[0] // 256
    lower = len_ref[0] - upper * 256
    stats = mine_ref[WIDTH + HALF : PAIR, :].astype(F32) + got_ref[WIDTH + HALF : PAIR, :].astype(F32)
    loss_high, loss_low = high_low(stats[0:1] + stats[1:2])
    tail = jnp.concatenate(
        [
            jnp.full((1, TOK), upper.astype(F32)),
            jnp.full((1, TOK), lower.astype(F32)),
            loss_high,
            loss_low,
            jnp.zeros((PAD - STAT - 4, TOK), F32),
        ],
        axis=0,
    )
    part = COLS // 4
    for d in range(SAMPLES):
        at = d * COLS
        rest = [acc[at + i * part : at + (i + 1) * part, 2 * TOK : HALF] for i in range(4)]
        block = [
            acc[at : at + COLS, 0:TOK],
            acc[at : at + COLS, TOK : 2 * TOK],
            jnp.concatenate(rest, axis=1),
            tail,
        ]
        out_ref[d] = jnp.concatenate(block, axis=0).astype(BF16)


def backward_kernel(
    own_ref,
    other_ref,
    attn_ref,
    back_ref,
    probs_ref,
    inv_ref,
    query_out,
    own_out,
    other_out,
    value_sc,
    key_sc,
    key_acc,
    value_acc,
    probs_sc,
    sems,
):
    blocks = SEQ // 2 // QB
    copies = [pltpu.make_async_copy(probs_ref.at[b], probs_sc.at[b], sems.at[b]) for b in range(blocks)]
    for copy in copies:
        copy.start()
    for side, ref in enumerate((own_ref, other_ref)):
        for c in range(CHIPS):
            at = (side * CHIPS + c) * TOK
            value_sc[at : at + TOK, :] = ref[c, 2 * HD : 3 * HD, :].astype(F32).T.astype(BF16)
            key_sc[:, at : at + TOK] = ref[c, HD : 2 * HD, :]
    for b in range(SEQ // 2 // QB):
        pair = QB // TOK
        chips = range(b * pair, (b + 1) * pair)
        query = jnp.concatenate([own_ref[c, 0:HD, :] for c in chips], axis=1)
        attn = jnp.concatenate([attn_ref[c] for c in chips], axis=1)
        back = jnp.concatenate([back_ref[c] for c in chips], axis=1)
        back = (back.astype(F32) * inv_ref[b : b + 1, :]).astype(BF16)
        delta = jnp.sum(back.astype(F32) * attn.astype(F32), axis=0, keepdims=True)
        copies[b].wait()
        probs = probs_sc[b]
        dprobs = dot(value_sc[...], back, NN)
        dscores = (probs.astype(F32) * (dprobs - delta)).astype(BF16)
        query_grad = dot(key_sc[...], dscores, NN).astype(BF16)
        for i, c in enumerate(chips):
            query_out[c] = query_grad[:, i * TOK : (i + 1) * TOK]
        key_part = dot(query, dscores, NT)
        value_part = dot(back, probs, NT)
        if b == 0:
            key_acc[...] = key_part
            value_acc[...] = value_part
        else:
            key_acc[...] += key_part
            value_acc[...] += value_part
    for side, ref in enumerate((own_out, other_out)):
        for c in range(CHIPS):
            at = (side * CHIPS + c) * TOK
            ref[c, 0:HD, :] = key_acc[:, at : at + TOK].astype(BF16)
            ref[c, HD : 2 * HD, :] = value_acc[:, at : at + TOK].astype(BF16)


def join_kernel(query_ref, own_ref, other_ref, out_ref):
    out_ref[:, 0:HD, :] = query_ref[...]
    out_ref[:, HD : 3 * HD, :] = (own_ref[...].astype(F32) + other_ref[...].astype(F32)).astype(BF16)


def reduce_kernel(part_ref, join_ref, out_ref, stat_ref, last_sc, sem):
    del join_ref
    total = part_ref[0].astype(F32)
    for d in range(1, SAMPLES):
        total = total + part_ref[d].astype(F32)
    count = 256.0 * total[STAT : STAT + 1] + total[STAT + 1 : STAT + 2]
    stat_ref[...] = jnp.broadcast_to(count, (8, TOK))
    loss = total[STAT + 2 : STAT + 3] + total[STAT + 3 : STAT + 4]
    tail = jnp.concatenate([*high_low(loss), jnp.zeros((2, TOK), F32)], axis=0)
    rest = total[2 * COLS : STAT]
    width = HALF - 2 * TOK
    rest = jnp.concatenate([rest[:, i * width : (i + 1) * width] for i in range(4)], axis=0)
    rest = jnp.concatenate([rest, jnp.zeros((COLS, TOK - width), F32)], axis=1)
    block = jnp.concatenate([total[0:COLS], total[COLS : 2 * COLS], rest], axis=1)
    turned = jnp.concatenate([block, jnp.zeros((TOK - COLS, 3 * TOK), F32)], axis=0).T
    for c in range(CHIPS):
        block = jnp.concatenate([turned[c * ROWS : (c + 1) * ROWS, :], tail], axis=0)
        last_sc[c] = block.astype(BF16)
    copy = pltpu.make_async_copy(last_sc, out_ref.at[:, 3 * HD : 3 * HD + LAST, :], sem)
    copy.start()
    copy.wait()


def unpack_kernel(rows_ref, stat_ref, query_ref, key_ref, value_ref, weight_ref, loss_ref):
    count = stat_ref[0:1, :]
    ratio = float(SAMPLES * SEQ) / count
    for at, (ref, factor) in enumerate(((query_ref, SCALE), (key_ref, SCALE), (value_ref, 1.0))):
        for h in range(HEADS):
            rows = rows_ref[h, at * HD : (at + 1) * HD, :].astype(F32)
            ref[0, h * HD : (h + 1) * HD, :] = rows * (ratio * factor)
    total = sum(rows_ref[c, 3 * HD : 3 * HD + LAST, :].astype(F32) for c in range(CHIPS))
    weight_ref[...] = (total[0:ROWS, :] * (ratio / SEQ))[:, 0:COLS]
    loss = jnp.sum(total[ROWS : ROWS + 1, :] + total[ROWS + 1 : ROWS + 2, :], axis=1, keepdims=True)
    loss_ref[...] = loss / (count[:, 0:1] * WIDTH)


def in_hbm(value):
    return pltpu.with_memory_space_constraint(value, pltpu.HBM)


def exchange(value, axis):
    return lax.all_to_all(value, axis, 0, 0, tiled=True)


def swap(value):
    return lax.ppermute(value, "patch_1", [(0, 1), (1, 0)])


def shape(dims, dtype):
    return jax.ShapeDtypeStruct(dims, dtype)


def local(query_rows, key_rows, value_rows, out_weight, target, lengths, segments):
    buffer = shape((CHIPS, BUF, TOK), BF16)
    heads = shape((CHIPS, HD, TOK), BF16)
    turned = [
        in_hbm(jnp.swapaxes(rows, 1, 2).reshape(HEADS, HD, TOK))
        for rows in (query_rows, key_rows, value_rows)
    ]
    packed = call(
        pack_kernel,
        buffer,
        [HB] * 4,
        10**6,
        10**6,
        [pltpu.VMEM((1, TOK), jnp.int32), pltpu.SemaphoreType.DMA((4,))],
        2,
    )(*turned, in_hbm(segments))
    own = exchange(packed, "patch_0")
    other = swap(own)
    blocks = SEQ // 2 // QB
    attn, probs, inv = call(
        forward_kernel,
        (heads, pltpu.HBM((blocks, SEQ, QB), BF16), shape((blocks, QB), F32)),
        [SM, VM, VM],
        4 * HD * SEQ * SEQ // 2,
        6 * 10**6,
        [
            pltpu.VMEM((SEQ, HD), BF16),
            pltpu.VMEM((SEQ, TOK), F32),
            pltpu.VMEM((HD, SEQ), BF16),
            pltpu.VMEM((blocks, SEQ, QB), BF16),
            pltpu.SemaphoreType.DMA((blocks,)),
        ],
        24,
        (VM, HB, VM),
    )(lengths, own, other)
    attn_rows = exchange(attn, "patch_0")
    back, grad_out, loss_part = call(
        project_kernel,
        (heads, shape((WIDTH, TOK), BF16), shape((1, TOK), F32)),
        [SM, VM, VM, VM],
        4 * TOK * FEAT * WIDTH,
        3 * 10**6,
    )(lengths, attn_rows, out_weight, target)
    back_heads = exchange(back, "patch_0")
    mine, half = call(
        pair_kernel, (shape((PAIR, TOK), BF16), shape((HALF, TOK), BF16)), [VM] * 3, 10**6, 10**6
    )(attn_rows, grad_out, loss_part)
    got_pair = swap(mine)
    weight_part = call(
        weight_kernel,
        shape((SAMPLES, PAD, TOK), BF16),
        [SM, VM, VM, VM],
        2 * TOK * FEAT * WIDTH,
        3 * 10**6,
        [pltpu.VMEM((WIDTH, 3 * TOK), F32)],
    )(lengths, mine, got_pair, half)
    weight_parts = exchange(weight_part, DP)
    pair = shape((CHIPS, 2 * HD, TOK), BF16)
    query_grad, own_grad, other_grad = call(
        backward_kernel,
        (heads, pair, pair),
        [VM, VM, VM, VM, HB, VM],
        8 * HD * SEQ * SEQ // 2,
        6 * 10**6,
        [
            pltpu.VMEM((SEQ, HD), BF16),
            pltpu.VMEM((HD, SEQ), BF16),
            pltpu.VMEM((HD, SEQ), F32),
            pltpu.VMEM((HD, SEQ), F32),
            pltpu.VMEM((blocks, SEQ, QB), BF16),
            pltpu.SemaphoreType.DMA((blocks,)),
        ],
        24,
    )(own, other, attn, back_heads, in_hbm(probs), inv)
    got = swap(other_grad)
    both = shape((CHIPS, 3 * HD + LAST, TOK), BF16)
    joined = call(join_kernel, both, [VM] * 3, 10**6, 10**6)(query_grad, own_grad, got)
    joined, stats = call(
        reduce_kernel,
        (both, shape((8, TOK), F32)),
        [VM, ANY],
        10**6,
        10**6,
        [pltpu.VMEM((CHIPS, LAST, TOK), BF16), pltpu.SemaphoreType.DMA],
        outs=(ANY, VM),
        aliases={1: 0},
    )(weight_parts, joined)
    grads = exchange(joined, "patch_0")
    rows = shape((1, FEAT, TOK), F32)
    query_out, key_out, value_out, weight_grad, loss = call(
        unpack_kernel,
        (rows, rows, rows, shape((ROWS, COLS), F32), shape((1, 1), F32)),
        [VM, VM],
        10**6,
        10**6,
    )(grads, stats)
    grads_out = (jnp.swapaxes(rows, 1, 2) for rows in (query_out, key_out, value_out))
    return *grads_out, weight_grad, loss[0, 0]


def solution(mesh):
    torus = Mesh(mesh.devices.reshape(4, 8, 8, 2), ("dp_0", "dp_1", "patch_0", "patch_1"))
    return jax.shard_map(
        local,
        mesh=torus,
        in_specs=(
            P(DP, PATCH, None),
            P(DP, PATCH, None),
            P(DP, PATCH, None),
            P(),
            P(DP, PATCH, None),
            P(DP),
            P(DP, PATCH),
        ),
        out_specs=(P(DP, PATCH, None), P(DP, PATCH, None), P(DP, PATCH, None), P(PATCH, DP), P()),
        check_vma=False,
    )
```

time: 150 us -> 119 us (0.79)
  the two profiles are of different devices: /device:TPU:1 before, /device:TPU:64 now
where the time goes in v2:
time: 119 us
  blocking collectives  53.5 us (45%)
  waiting for transfers between devices  22.7 us (19%)
  starting transfers between devices  21.7 us (18%)
  Pallas kernels  19.3 us (16%)
  between operations  1.39 us (1%)
    all_to_all x3, blocking collectives, exchange(): return lax.all_to_all(value, axis, 0, 0, tiled=True)  53.5 us
    all_to_all x2, waiting for transfers between devices, exchange(): return lax.all_to_all(value, axis, 0, 0, tiled=True)  20 us
    all_to_all x2, starting transfers between devices, exchange(): return lax.all_to_all(value, axis, 0, 0, tiled=True)  16 us
    pallas_call x1, Pallas kernels, local(): call(backward_kernel, (heads, pair, pair), [VM, VM, VM, VM, HB, VM], 8 *...  7.15 us
    pallas_call x1, Pallas kernels, local(): call(forward_kernel, (heads, pltpu.HBM((blocks, SEQ, QB), BF16), shape((b...  6.52 us
    ppermute x3, starting transfers between devices, swap(): return lax.ppermute(value, 'patch_1', [(0, 1), (1, 0)])  5.75 us
    ppermute x3, waiting for transfers between devices, swap(): return lax.ppermute(value, 'patch_1', [(0, 1), (1, 0)])  2.69 us
  transfers between devices with their start and end apart: 5, of which 4 were waited for; matrix products, arithmetic and copies ran while one was open for 0% of the time, Pallas kernels for 7%

profile of v2, /device:TPU:64, one launch (start us, length us, event | category | flops | bytes accessed | tf_op | source)
XLA Modules:
  0.0 118.7 jit_solution(11041988231728758104)
XLA Ops:
  0.6 0.0 copy-start
  0.6 0.0 copy-start.1
  0.7 1.2 %shard_map.110 = bf16[8,224,128]{2,1,0:T(8,128)(2,1)S(1)} custom-call(bf16[8,72,128]{2,1,0:T(8,128)(2,1)} %bitcast.13, bf16[8,72,128]{2,1,0:T(8,128)(2,1)} %bitcast.14, bf16[8,72,128]{2,1,0:T(8,128)(2,1)} %bitcast.15, s32[1,128]{1,0:T(1,128)} %seg_ref.1), custom_call_target="tpu_custom_call" | custom-call | flops 1000000 | bytes 1000000 | tf_op jit(solution)/shard_map/pallas_call | solution.py:310
  1.9 23.0 %all_to_all.25.own_ref = bf16[8,224,128]{2,1,0:T(8,128)(2,1)S(1)} all-to-all(bf16[8,224,128]{2,1,0:T(8,128)(2,1)S(1)} %shard_map.110), channel_id=1, replica_groups=mesh['dp_0'=4,'dp_1'=8,'patch_0'=8,'patch_1'=2] {'patch_0'}, dimensions={0} | all-to-all | bytes 917504 | tf_op jit(solution)/shard_map/all_to_all | solution.py:292
  24.9 1.9 %collective-permute-start = (bf16[8,224,128]{2,1,0:T(8,128)(2,1)S(1)}, bf16[8,224,128]{2,1,0:T(8,128)(2,1)S(1)}, u32[]{:S(2)}, u32[]{:S(2)}) collective-permute-start(bf16[8,224,128]{2,1,0:T(8,128)(2,1)S(1)} %all_to_all.25.own_ref), channel_id=1, source_target_pairs={{0,1},{1,0},{2,3},{3,2},{4,5},{5,4},{6,7},{7,6},{8,9},{9,8},{10,11... | collective-permute-start | bytes 1376264 | tf_op jit(solution)/shard_map/ppermute | solution.py:296
  27.4 1.1 collective-permute-done.other_ref
  28.6 6.5 %shard_map.111 = (bf16[8,72,128]{2,1,0:T(8,128)(2,1)S(1)}, bf16[4,2048,256]{2,1,0:T(8,128)(2,1)}, f32[4,256]{1,0:T(4,128)S(1)}) custom-call(s32[1]{0:T(128)S(6)} %copy.14.len_ref, bf16[8,224,128]{2,1,0:T(8,128)(2,1)S(1)} %all_to_all.25.own_ref, bf16[8,224,128]{2,1,0:T(8,128)(2,1)S(1)} %collective-permute-done.other_ref), custom_call_target="tpu_custom_call" | custom-call | flops 603979776 | bytes 6000000 | tf_op jit(solution)/shard_map/pallas_call | solution.py:322
  35.1 12.4 %all_to_all.26.attn_ref = bf16[8,72,128]{2,1,0:T(8,128)(2,1)S(1)} all-to-all(bf16[8,72,128]{2,1,0:T(8,128)(2,1)S(1)} %get-tuple-element.23.attn_ref), channel_id=1, replica_groups=mesh['dp_0'=4,'dp_1'=8,'patch_0'=8,'patch_1'=2] {'patch_0'}, dimensions={0} | all-to-all | bytes 294912 | tf_op jit(solution)/shard_map/all_to_all | solution.py:292
  47.5 0.0 copy-done
  47.5 0.0 copy-done.1
  47.5 1.6 %shard_map.112 = (bf16[8,72,128]{2,1,0:T(8,128)(2,1)}, bf16[1152,128]{1,0:T(8,128)(2,1)S(1)}, f32[1,128]{1,0:T(1,128)S(1)}) custom-call(s32[1]{0:T(128)S(6)} %copy.14.len_ref, bf16[8,72,128]{2,1,0:T(8,128)(2,1)S(1)} %all_to_all.26.attn_ref, bf16[576,1152]{1,0:T(8,128)(2,1)S(1)} %copy-done, bf16[1,128,1152]{2,1,0:T(8,128)(2,1)S(1)} %copy-done.1), custom_call_target="tpu_custom_call" | custom-call | flops 339738624 | bytes 3000000 | tf_op jit(solution)/shard_map/pallas_call | solution.py:339
  49.1 0.1 shard_map.113
  49.2 1.9 %collective-permute-start.1 = (bf16[1448,128]{1,0:T(8,128)(2,1)S(1)}, bf16[1448,128]{1,0:T(8,128)(2,1)S(1)}, u32[]{:S(2)}, u32[]{:S(2)}) collective-permute-start(bf16[1448,128]{1,0:T(8,128)(2,1)S(1)} %get-tuple-element.26.mine_ref), channel_id=1, source_target_pairs={{0,1},{1,0},{2,3},{3,2},{4,5},{5,4},{6,7},{7,6},{8,9},{9,8},{10,11... | collective-permute-start | bytes 1112072 | tf_op jit(solution)/shard_map/ppermute | solution.py:296
  51.1 3.4 %all-to-all-start.3 = ((bf16[8,72,128]{2,1,0:T(8,128)(2,1)}), bf16[8,72,128]{2,1,0:T(8,128)(2,1)S(1)}, u32[]{:S(2)}, u32[]{:S(2)}) async-start(bf16[8,72,128]{2,1,0:T(8,128)(2,1)} %get-tuple-element.28), calls=%async_computation.3 | async-start | bytes 294912 | tf_op jit(solution)/shard_map/all_to_all | solution.py:292
  54.5 0.0 collective-permute-done.1.got_ref
  54.5 1.5 %shard_map.114 = bf16[32,88,128]{2,1,0:T(8,128)(2,1)} custom-call(s32[1]{0:T(128)S(6)} %copy.14.len_ref, bf16[1448,128]{1,0:T(8,128)(2,1)S(1)} %get-tuple-element.26.mine_ref, bf16[1448,128]{1,0:T(8,128)(2,1)S(1)} %collective-permute-done.1.got_ref, bf16[288,128]{1,0:T(8,128)(2,1)S(1)} %get-tuple-element.27.half_ref), custom_call_target="tpu_custom_call" | custom-call | flops 169869312 | bytes 3000000 | tf_op jit(solution)/shard_map/pallas_call | solution.py:351
  56.0 8.8 %all-to-all-done.3.back_ref = bf16[8,72,128]{2,1,0:T(8,128)(2,1)S(1)} async-done(((bf16[8,72,128]{2,1,0:T(8,128)(2,1)}), bf16[8,72,128]{2,1,0:T(8,128)(2,1)S(1)}, u32[]{:S(2)}, u32[]{:S(2)}) %all-to-all-start.3) | async-done | bytes 147488 | tf_op jit(solution)/shard_map/all_to_all | solution.py:292
  64.8 12.6 %all-to-all-start.2 = ((bf16[32,88,128]{2,1,0:T(8,128)(2,1)}), bf16[32,88,128]{2,1,0:T(8,128)(2,1)S(1)}, u32[]{:S(2)}, u32[]{:S(2)}) async-start(bf16[32,88,128]{2,1,0:T(8,128)(2,1)} %shard_map.114), calls=%async_computation.2 | async-start | bytes 1441792 | tf_op jit(solution)/shard_map/all_to_all | solution.py:292
  77.4 7.1 %shard_map.115 = (bf16[8,72,128]{2,1,0:T(8,128)(2,1)S(1)}, bf16[8,144,128]{2,1,0:T(8,128)(2,1)S(1)}, bf16[8,144,128]{2,1,0:T(8,128)(2,1)S(1)}) custom-call(bf16[8,224,128]{2,1,0:T(8,128)(2,1)S(1)} %all_to_all.25.own_ref, bf16[8,224,128]{2,1,0:T(8,128)(2,1)S(1)} %collective-permute-done.other_ref, bf16[8,72,128]{2,1,0:T(8,128)(2,1)S(1)} %get-tuple-element.23.attn_ref, ...), custom_call_target="tpu_custom_call" | custom-call | flops 1207959552 | bytes 6000000 | tf_op jit(solution)/shard_map/pallas_call | solution.py:361
  84.5 1.9 %collective-permute-start.2 = (bf16[8,144,128]{2,1,0:T(8,128)(2,1)S(1)}, bf16[8,144,128]{2,1,0:T(8,128)(2,1)S(1)}, u32[]{:S(2)}, u32[]{:S(2)}) collective-permute-start(bf16[8,144,128]{2,1,0:T(8,128)(2,1)S(1)} %get-tuple-element.33), channel_id=1, source_target_pairs={{0,1},{1,0},{2,3},{3,2},{4,5},{5,4},{6,7},{7,6},{8,9},{9,8},{10,11... | collective-permute-start | bytes 884744 | tf_op jit(solution)/shard_map/ppermute | solution.py:296
  86.4 1.5 %collective-permute-done.2.other_ref = bf16[8,144,128]{2,1,0:T(8,128)(2,1)S(1)} collective-permute-done((bf16[8,144,128]{2,1,0:T(8,128)(2,1)S(1)}, bf16[8,144,128]{2,1,0:T(8,128)(2,1)S(1)}, u32[]{:S(2)}, u32[]{:S(2)}) %collective-permute-start.2) | collective-permute-done | bytes 294944 | tf_op jit(solution)/shard_map/ppermute | solution.py:296
  88.0 0.1 shard_map.116.join_ref
  88.1 11.2 %all-to-all-done.2.part_ref = bf16[32,88,128]{2,1,0:T(8,128)(2,1)S(1)} async-done(((bf16[32,88,128]{2,1,0:T(8,128)(2,1)}), bf16[32,88,128]{2,1,0:T(8,128)(2,1)S(1)}, u32[]{:S(2)}, u32[]{:S(2)}) %all-to-all-start.2) | async-done | bytes 720928 | tf_op jit(solution)/shard_map/all_to_all | solution.py:292
  99.3 0.2 shard_map.117
  99.5 18.2 %all_to_all.27.rows_ref = bf16[8,256,128]{2,1,0:T(8,128)(2,1)S(1)} all-to-all(bf16[8,256,128]{2,1,0:T(8,128)(2,1)S(1)} %get-tuple-element.34), channel_id=1, replica_groups=mesh['dp_0'=4,'dp_1'=8,'patch_0'=8,'patch_1'=2] {'patch_0'}, dimensions={0} | all-to-all | bytes 1048576 | tf_op jit(solution)/shard_map/all_to_all | solution.py:292
  117.7 0.9 shard_map.118
Async XLA Ops:
  0.6 46.8 %copy-start = (bf16[576,1152]{1,0:T(8,128)(2,1)S(1)}, bf16[576,1152]{1,0:T(8,128)(2,1)}, u32[]{:S(2)}) copy-start(bf16[576,1152]{1,0:T(8,128)(2,1)} %weight_ref.1) | copy-start | bytes 3981316
  0.6 46.8 %copy-start.1 = (bf16[1,128,1152]{2,1,0:T(8,128)(2,1)S(1)}, bf16[1,128,1152]{2,1,0:T(8,128)(2,1)}, u32[]{:S(2)}) copy-start(bf16[1,128,1152]{2,1,0:T(8,128)(2,1)} %target_ref.1) | copy-start | bytes 884740
  24.9 3.7 %collective-permute-start = (bf16[8,224,128]{2,1,0:T(8,128)(2,1)S(1)}, bf16[8,224,128]{2,1,0:T(8,128)(2,1)S(1)}, u32[]{:S(2)}, u32[]{:S(2)}) collective-permute-start(bf16[8,224,128]{2,1,0:T(8,128)(2,1)S(1)} %all_to_all.25.own_ref), channel_id=1, source_target_pairs={{0,1},{1,0},{2,3},{3,2},{4,5},{5,4},{6,7},{7,6},{8,9},{9,8},{10,11... | collective-permute-start | bytes 1376264 | tf_op jit(solution)/shard_map/ppermute | solution.py:296
  49.2 5.3 %collective-permute-start.1 = (bf16[1448,128]{1,0:T(8,128)(2,1)S(1)}, bf16[1448,128]{1,0:T(8,128)(2,1)S(1)}, u32[]{:S(2)}, u32[]{:S(2)}) collective-permute-start(bf16[1448,128]{1,0:T(8,128)(2,1)S(1)} %get-tuple-element.26.mine_ref), channel_id=1, source_target_pairs={{0,1},{1,0},{2,3},{3,2},{4,5},{5,4},{6,7},{7,6},{8,9},{9,8},{10,11... | collective-permute-start | bytes 1112072 | tf_op jit(solution)/shard_map/ppermute | solution.py:296
  51.1 13.7 %all-to-all-start.3 = ((bf16[8,72,128]{2,1,0:T(8,128)(2,1)}), bf16[8,72,128]{2,1,0:T(8,128)(2,1)S(1)}, u32[]{:S(2)}, u32[]{:S(2)}) async-start(bf16[8,72,128]{2,1,0:T(8,128)(2,1)} %get-tuple-element.28), calls=%async_computation.3 | async-start | bytes 294912 | tf_op jit(solution)/shard_map/all_to_all | solution.py:292
  64.8 34.5 %all-to-all-start.2 = ((bf16[32,88,128]{2,1,0:T(8,128)(2,1)}), bf16[32,88,128]{2,1,0:T(8,128)(2,1)S(1)}, u32[]{:S(2)}, u32[]{:S(2)}) async-start(bf16[32,88,128]{2,1,0:T(8,128)(2,1)} %shard_map.114), calls=%async_computation.2 | async-start | bytes 1441792 | tf_op jit(solution)/shard_map/all_to_all | solution.py:292
  84.5 3.5 %collective-permute-start.2 = (bf16[8,144,128]{2,1,0:T(8,128)(2,1)S(1)}, bf16[8,144,128]{2,1,0:T(8,128)(2,1)S(1)}, u32[]{:S(2)}, u32[]{:S(2)}) collective-permute-start(bf16[8,144,128]{2,1,0:T(8,128)(2,1)S(1)} %get-tuple-element.33), channel_id=1, source_target_pairs={{0,1},{1,0},{2,3},{3,2},{4,5},{5,4},{6,7},{7,6},{8,9},{9,8},{10,11... | collective-permute-start | bytes 884744 | tf_op jit(solution)/shard_map/ppermute | solution.py:296

commit v3 on v2

--- a/solution.py
+++ b/solution.py
@@ -23,10 +23,15 @@
 HALF = FEAT // 2
 STAT = COLS * HALF // TOK
 PAD = 88
-LAST = ROWS + 4
+THIRD = ROWS // 3
+LAST = 16
+DEPTH = 8
 PAIR = WIDTH + HALF + 8
 BUF = 3 * HD + 8
 QB = 256
+KEYS = 256
+NEAR = 1
+FAR = SEQ // 2 // QB - NEAR
 NEG_LARGE = -1e30
 SCALE = 1.0 / math.sqrt(HD)
 EXP2_SCALE = SCALE * math.log2(math.e)
@@ -85,12 +90,12 @@
 
 
 def forward_kernel(
-    len_ref, own_ref, other_ref, attn_ref, probs_ref, inv_ref, key_sc, group_sc, value_sc, probs_sc, sems
+    len_ref, own_ref, other_ref, attn_ref, near_ref, far_ref, inv_ref, key_sc, group_sc, value_sc, far_sc, sems, *score_refs
 ):
     core = lax.axis_index("patch_1")
     length = len_ref[0]
     own_groups = []
-    copies = []
+    copies = [pltpu.make_async_copy(far_sc.at[i], far_ref.at[i], sems.at[i]) for i in range(FAR)]
     for side, ref in enumerate((own_ref, other_ref)):
         for c in range(CHIPS):
             at = (side * CHIPS + c) * TOK
@@ -100,24 +105,44 @@
             if side == 0:
                 own_groups.append(group)
             group_sc[at : at + TOK, :] = jnp.broadcast_to(group, (TOK, TOK)).T
-    for b in range(SEQ // 2 // QB):
-        pair = QB // TOK
-        query = jnp.concatenate([own_ref[b * pair + i, 0:HD, :] for i in range(pair)], axis=1)
-        group = jnp.concatenate([own_groups[b * pair + i] for i in range(pair)], axis=1)
-        scores = dot(key_sc[...], query, NN)
-        key_group = jnp.concatenate([group_sc[...]] * pair, axis=1)
-        masked = jnp.where(key_group == group, scores, NEG_LARGE)
-        top = jnp.max(masked, axis=0, keepdims=True)
-        probs = jnp.exp2((masked - top) * EXP2_SCALE)
-        inv = 1.0 / jnp.sum(probs, axis=0, keepdims=True)
-        weights = probs.astype(BF16)
-        probs_sc[b] = weights
-        copies.append(pltpu.make_async_copy(probs_sc.at[b], probs_ref.at[b], sems.at[b]))
-        copies[b].start()
-        attn = (dot(value_sc[...], weights, NN) * inv).astype(BF16)
-        inv_ref[b : b + 1, :] = inv
-        for i in range(pair):
-            attn_ref[b * pair + i] = attn[:, i * TOK : (i + 1) * TOK]
+    order = (*range(NEAR, NEAR + FAR), *range(NEAR))
+    pair = QB // TOK
+    held = None
+    for step in range(len(order) + 1):
+        scores = score_refs[step % 2]
+        if step < len(order):
+            chips = range(order[step] * pair, (order[step] + 1) * pair)
+            query = jnp.concatenate([own_ref[c, 0:HD, :] for c in chips], axis=1)
+            group = jnp.concatenate([own_groups[c] for c in chips], axis=1)
+            top = jnp.full((8, QB), NEG_LARGE, F32)
+        if held is not None:
+            b, held_scores, held_top = held
+            weights_ref = near_ref.at[b] if b < NEAR else far_sc.at[b - NEAR]
+            denom = jnp.zeros((8, QB), F32)
+            accum = jnp.zeros((HD, QB), F32)
+        for j in range(SEQ // KEYS):
+            rows = slice(j * KEYS, (j + 1) * KEYS)
+            if step < len(order):
+                key_group = jnp.concatenate([group_sc[rows, :]] * pair, axis=1)
+                masked = jnp.where(key_group == group, dot(key_sc[rows, :], query, NN), NEG_LARGE)
+                scores[rows, :] = masked
+                top = jnp.maximum(top, jnp.max(masked.reshape(KEYS // 8, 8, QB), axis=0))
+            if held is not None:
+                probs = jnp.exp2((held_scores[rows, :] - held_top) * EXP2_SCALE)
+                denom = denom + jnp.sum(probs.reshape(KEYS // 8, 8, QB), axis=0)
+                weights = probs.astype(BF16)
+                weights_ref[rows, :] = weights
+                accum = accum + dot(value_sc[:, rows], weights, NN)
+        if held is not None:
+            if b >= NEAR:
+                copies[b - NEAR].start()
+            inv = 1.0 / jnp.sum(denom, axis=0, keepdims=True)
+            attn = (accum * inv).astype(BF16)
+            inv_ref[b : b + 1, :] = inv
+            for i in range(pair):
+                attn_ref[b * pair + i] = attn[:, i * TOK : (i + 1) * TOK]
+        if step < len(order):
+            held = (order[step], scores, jnp.max(top, axis=0, keepdims=True))
     for copy in copies:
         copy.wait()
 
@@ -156,24 +181,23 @@
     pair_ref[WIDTH + HALF : PAIR, :] = stats.astype(BF16)
 
 
+def stat_rows(count, loss):
+    upper = jnp.floor(count * (1.0 / 256.0))
+    rows = [upper, count - 256.0 * upper, *high_low(loss), jnp.zeros((PAD - STAT - 4, TOK), F32)]
+    return jnp.concatenate(rows, axis=0)
+
+
+def stats_of(block):
+    count = 256.0 * block[STAT : STAT + 1] + block[STAT + 1 : STAT + 2]
+    return count, block[STAT + 2 : STAT + 3] + block[STAT + 3 : STAT + 4]
+
+
 def weight_kernel(len_ref, mine_ref, got_ref, half_ref, out_ref, acc):
     left = jnp.concatenate([mine_ref[0:WIDTH, :], got_ref[0:WIDTH, :]], axis=1)
     right = jnp.concatenate([half_ref[...], got_ref[WIDTH : WIDTH + HALF, :]], axis=1)
     acc[:, 0:HALF] = dot(left, right, NT)
-    upper = len_ref[0] // 256
-    lower = len_ref[0] - upper * 256
     stats = mine_ref[WIDTH + HALF : PAIR, :].astype(F32) + got_ref[WIDTH + HALF : PAIR, :].astype(F32)
-    loss_high, loss_low = high_low(stats[0:1] + stats[1:2])
-    tail = jnp.concatenate(
-        [
-            jnp.full((1, TOK), upper.astype(F32)),
-            jnp.full((1, TOK), lower.astype(F32)),
-            loss_high,
-            loss_low,
-            jnp.zeros((PAD - STAT - 4, TOK), F32),
-        ],
-        axis=0,
-    )
+    tail = stat_rows(jnp.full((1, TOK), len_ref[0].astype(F32)), stats[0:1] + stats[1:2])
     part = COLS // 4
     for d in range(SAMPLES):
         at = d * COLS
@@ -184,7 +208,17 @@
             jnp.concatenate(rest, axis=1),
             tail,
         ]
-        out_ref[d] = jnp.concatenate(block, axis=0).astype(BF16)
+        out_ref[d // DEPTH, d % DEPTH] = jnp.concatenate(block, axis=0).astype(BF16)
+
+
+def sum_kernel(part_ref, out_ref):
+    total = part_ref[0].astype(F32)
+    for x in range(1, SAMPLES // DEPTH):
+        total = total + part_ref[x].astype(F32)
+    out_ref[...] = total.astype(BF16)
+    tail = stat_rows(*stats_of(total[0])).astype(BF16)
+    for z in range(DEPTH):
+        out_ref[z, STAT:PAD, :] = tail
 
 
 def backward_kernel(
@@ -192,7 +226,8 @@
     other_ref,
     attn_ref,
     back_ref,
-    probs_ref,
+    near_ref,
+    far_ref,
     inv_ref,
     query_out,
     own_out,
@@ -201,11 +236,10 @@
     key_sc,
     key_acc,
     value_acc,
-    probs_sc,
+    far_sc,
     sems,
 ):
-    blocks = SEQ // 2 // QB
-    copies = [pltpu.make_async_copy(probs_ref.at[b], probs_sc.at[b], sems.at[b]) for b in range(blocks)]
+    copies = [pltpu.make_async_copy(far_ref.at[i], far_sc.at[i], sems.at[i]) for i in range(FAR)]
     for copy in copies:
         copy.start()
     for side, ref in enumerate((own_ref, other_ref)):
@@ -221,8 +255,10 @@
         back = jnp.concatenate([back_ref[c] for c in chips], axis=1)
         back = (back.astype(F32) * inv_ref[b : b + 1, :]).astype(BF16)
         delta = jnp.sum(back.astype(F32) * attn.astype(F32), axis=0, keepdims=True)
-        copies[b].wait()
-        probs = probs_sc[b]
+        if b == NEAR:
+            for copy in copies:
+                copy.wait()
+        probs = near_ref[b] if b < NEAR else far_sc[b - NEAR]
         dprobs = dot(value_sc[...], back, NN)
         dscores = (probs.astype(F32) * (dprobs - delta)).astype(BF16)
         query_grad = dot(key_sc[...], dscores, NN).astype(BF16)
@@ -251,21 +287,21 @@
 def reduce_kernel(part_ref, join_ref, out_ref, stat_ref, last_sc, sem):
     del join_ref
     total = part_ref[0].astype(F32)
-    for d in range(1, SAMPLES):
+    for d in range(1, DEPTH):
         total = total + part_ref[d].astype(F32)
-    count = 256.0 * total[STAT : STAT + 1] + total[STAT + 1 : STAT + 2]
+    count, loss = stats_of(total)
     stat_ref[...] = jnp.broadcast_to(count, (8, TOK))
-    loss = total[STAT + 2 : STAT + 3] + total[STAT + 3 : STAT + 4]
-    tail = jnp.concatenate([*high_low(loss), jnp.zeros((2, TOK), F32)], axis=0)
     rest = total[2 * COLS : STAT]
     width = HALF - 2 * TOK
     rest = jnp.concatenate([rest[:, i * width : (i + 1) * width] for i in range(4)], axis=0)
     rest = jnp.concatenate([rest, jnp.zeros((COLS, TOK - width), F32)], axis=1)
     block = jnp.concatenate([total[0:COLS], total[COLS : 2 * COLS], rest], axis=1)
     turned = jnp.concatenate([block, jnp.zeros((TOK - COLS, 3 * TOK), F32)], axis=0).T
+    loss = jnp.concatenate([*high_low(loss), jnp.zeros((LAST - THIRD - 2, TOK), F32)], axis=0)
     for c in range(CHIPS):
-        block = jnp.concatenate([turned[c * ROWS : (c + 1) * ROWS, :], tail], axis=0)
-        last_sc[c] = block.astype(BF16)
+        thirds = [turned[c * ROWS + i * THIRD : c * ROWS + (i + 1) * THIRD, 0:COLS] for i in range(3)]
+        rows = jnp.concatenate([*thirds, jnp.zeros((THIRD, TOK - 3 * COLS), F32)], axis=1)
+        last_sc[c] = jnp.concatenate([rows, loss], axis=0).astype(BF16)
     copy = pltpu.make_async_copy(last_sc, out_ref.at[:, 3 * HD : 3 * HD + LAST, :], sem)
     copy.start()
     copy.wait()
@@ -279,8 +315,10 @@
             rows = rows_ref[h, at * HD : (at + 1) * HD, :].astype(F32)
             ref[0, h * HD : (h + 1) * HD, :] = rows * (ratio * factor)
     total = sum(rows_ref[c, 3 * HD : 3 * HD + LAST, :].astype(F32) for c in range(CHIPS))
-    weight_ref[...] = (total[0:ROWS, :] * (ratio / SEQ))[:, 0:COLS]
-    loss = jnp.sum(total[ROWS : ROWS + 1, :] + total[ROWS + 1 : ROWS + 2, :], axis=1, keepdims=True)
+    scaled = total * (ratio / SEQ)
+    thirds = [scaled[0:THIRD, i * COLS : (i + 1) * COLS] for i in range(3)]
+    weight_ref[...] = jnp.concatenate(thirds, axis=0)
+    loss = jnp.sum(total[THIRD : THIRD + 1] + total[THIRD + 1 : THIRD + 2], axis=1, keepdims=True)
     loss_ref[...] = loss / (count[:, 0:1] * WIDTH)
 
 
@@ -319,9 +357,9 @@
     own = exchange(packed, "patch_0")
     other = swap(own)
     blocks = SEQ // 2 // QB
-    attn, probs, inv = call(
+    attn, near, far, inv = call(
         forward_kernel,
-        (heads, pltpu.HBM((blocks, SEQ, QB), BF16), shape((blocks, QB), F32)),
+        (heads, shape((NEAR, SEQ, QB), BF16), pltpu.HBM((FAR, SEQ, QB), BF16), shape((blocks, QB), F32)),
         [SM, VM, VM],
         4 * HD * SEQ * SEQ // 2,
         6 * 10**6,
@@ -329,11 +367,13 @@
             pltpu.VMEM((SEQ, HD), BF16),
             pltpu.VMEM((SEQ, TOK), F32),
             pltpu.VMEM((HD, SEQ), BF16),
-            pltpu.VMEM((blocks, SEQ, QB), BF16),
-            pltpu.SemaphoreType.DMA((blocks,)),
+            pltpu.VMEM((FAR, SEQ, QB), BF16),
+            pltpu.SemaphoreType.DMA((FAR,)),
+            pltpu.VMEM((SEQ, QB), F32),
+            pltpu.VMEM((SEQ, QB), F32),
         ],
         24,
-        (VM, HB, VM),
+        (VM, VM, HB, VM),
     )(lengths, own, other)
     attn_rows = exchange(attn, "patch_0")
     back, grad_out, loss_part = call(
@@ -350,18 +390,18 @@
     got_pair = swap(mine)
     weight_part = call(
         weight_kernel,
-        shape((SAMPLES, PAD, TOK), BF16),
+        shape((SAMPLES // DEPTH, DEPTH, PAD, TOK), BF16),
         [SM, VM, VM, VM],
         2 * TOK * FEAT * WIDTH,
         3 * 10**6,
         [pltpu.VMEM((WIDTH, 3 * TOK), F32)],
     )(lengths, mine, got_pair, half)
-    weight_parts = exchange(weight_part, DP)
+    weight_rows = exchange(weight_part, "dp_0")
     pair = shape((CHIPS, 2 * HD, TOK), BF16)
     query_grad, own_grad, other_grad = call(
         backward_kernel,
         (heads, pair, pair),
-        [VM, VM, VM, VM, HB, VM],
+        [VM, VM, VM, VM, VM, HB, VM],
         8 * HD * SEQ * SEQ // 2,
         6 * 10**6,
         [
@@ -369,11 +409,13 @@
             pltpu.VMEM((HD, SEQ), BF16),
             pltpu.VMEM((HD, SEQ), F32),
             pltpu.VMEM((HD, SEQ), F32),
-            pltpu.VMEM((blocks, SEQ, QB), BF16),
-            pltpu.SemaphoreType.DMA((blocks,)),
+            pltpu.VMEM((FAR, SEQ, QB), BF16),
+            pltpu.SemaphoreType.DMA((FAR,)),
         ],
         24,
-    )(own, other, attn, back_heads, in_hbm(probs), inv)
+    )(own, other, attn, back_heads, near, in_hbm(far), inv)
+    weight_row = call(sum_kernel, shape((DEPTH, PAD, TOK), BF16), [VM], 10**6, 10**6)(weight_rows)
+    weight_parts = exchange(weight_row, "dp_1")
     got = swap(other_grad)
     both = shape((CHIPS, 3 * HD + LAST, TOK), BF16)
     joined = call(join_kernel, both, [VM] * 3, 10**6, 10**6)(query_grad, own_grad, got)

time: 119 us -> 120 us (level)
  the two profiles are of different devices: /device:TPU:64 before, /device:TPU:1 now
where the time goes in v3:
time: 120 us; the launch traced here: 119 us
  blocking collectives  65 us (54%)
  starting transfers between devices  26.6 us (22%)
  Pallas kernels  15.4 us (13%)
  waiting for transfers between devices  10.5 us (9%)
  between operations  1.39 us (1%)
    all_to_all x4, blocking collectives, exchange(): return lax.all_to_all(value, axis, 0, 0, tiled=True)  65 us
    all_to_all x2, starting transfers between devices, exchange(): return lax.all_to_all(value, axis, 0, 0, tiled=True)  13.4 us
    ppermute x3, starting transfers between devices, swap(): return lax.ppermute(value, 'patch_1', [(0, 1), (1, 0)])  13.2 us
    all_to_all x2, waiting for transfers between devices, exchange(): return lax.all_to_all(value, axis, 0, 0, tiled=True)  7.29 us
    pallas_call x1, Pallas kernels, local(): call(backward_kernel, (heads, pair, pair), [VM, VM, VM, VM, VM, HB, VM],...  5.44 us
    pallas_call x1, Pallas kernels, local(): call(forward_kernel, (heads, shape((NEAR, SEQ, QB), BF16), pltpu.HBM((FAR...  4.27 us
    ppermute x3, waiting for transfers between devices, swap(): return lax.ppermute(value, 'patch_1', [(0, 1), (1, 0)])  3.26 us
  transfers between devices with their start and end apart: 5, of which 4 were waited for; matrix products, arithmetic and copies ran while one was open for 0% of the time, Pallas kernels for 5%

profile of v3, /device:TPU:1, one launch (start us, length us, event | category | flops | bytes accessed | tf_op | source)
XLA Modules:
  0.0 118.9 jit_solution(4938900048247613804)
XLA Ops:
  0.6 0.0 copy-start
  0.6 0.0 copy-start.1
  0.7 1.2 %shard_map.110 = bf16[8,224,128]{2,1,0:T(8,128)(2,1)S(1)} custom-call(bf16[8,72,128]{2,1,0:T(8,128)(2,1)} %bitcast.13, bf16[8,72,128]{2,1,0:T(8,128)(2,1)} %bitcast.14, bf16[8,72,128]{2,1,0:T(8,128)(2,1)} %bitcast.15, s32[1,128]{1,0:T(1,128)} %seg_ref.1), custom_call_target="tpu_custom_call" | custom-call | flops 1000000 | bytes 1000000 | tf_op jit(solution)/shard_map/pallas_call | solution.py:348
  1.9 21.5 %all_to_all.30.own_ref = bf16[8,224,128]{2,1,0:T(8,128)(2,1)S(1)} all-to-all(bf16[8,224,128]{2,1,0:T(8,128)(2,1)S(1)} %shard_map.110), channel_id=1, replica_groups=mesh['dp_0'=4,'dp_1'=8,'patch_0'=8,'patch_1'=2] {'patch_0'}, dimensions={0} | all-to-all | bytes 917504 | tf_op jit(solution)/shard_map/all_to_all | solution.py:330
  23.4 4.9 %collective-permute-start = (bf16[8,224,128]{2,1,0:T(8,128)(2,1)S(1)}, bf16[8,224,128]{2,1,0:T(8,128)(2,1)S(1)}, u32[]{:S(2)}, u32[]{:S(2)}) collective-permute-start(bf16[8,224,128]{2,1,0:T(8,128)(2,1)S(1)} %all_to_all.30.own_ref), channel_id=1, source_target_pairs={{0,1},{1,0},{2,3},{3,2},{4,5},{5,4},{6,7},{7,6},{8,9},{9,8},{10,11... | collective-permute-start | bytes 1376264 | tf_op jit(solution)/shard_map/ppermute | solution.py:334
  28.9 0.8 collective-permute-done.other_ref
  29.7 4.3 %shard_map.111 = (bf16[8,72,128]{2,1,0:T(8,128)(2,1)S(1)}, bf16[1,2048,256]{2,1,0:T(8,128)(2,1)S(1)}, bf16[3,2048,256]{2,1,0:T(8,128)(2,1)}, f32[4,256]{1,0:T(4,128)S(1)}) custom-call(s32[1]{0:T(128)S(6)} %copy.14.len_ref, bf16[8,224,128]{2,1,0:T(8,128)(2,1)S(1)} %all_to_all.30.own_ref, bf16[8,224,128]{2,1,0:T(8,128)(2,1)S(1)} %collective-permute-done.other_ref), custom_call_target="tpu_custom_call" | custom-call | flops 603979776 | bytes 6000000 | tf_op jit(solution)/shard_map/pallas_call | solution.py:360
  34.0 11.1 %all_to_all.31.attn_ref = bf16[8,72,128]{2,1,0:T(8,128)(2,1)S(1)} all-to-all(bf16[8,72,128]{2,1,0:T(8,128)(2,1)S(1)} %get-tuple-element.24.attn_ref), channel_id=1, replica_groups=mesh['dp_0'=4,'dp_1'=8,'patch_0'=8,'patch_1'=2] {'patch_0'}, dimensions={0} | all-to-all | bytes 294912 | tf_op jit(solution)/shard_map/all_to_all | solution.py:330
  45.0 0.0 copy-done
  45.0 0.0 copy-done.1
  45.1 1.6 %shard_map.112 = (bf16[8,72,128]{2,1,0:T(8,128)(2,1)}, bf16[1152,128]{1,0:T(8,128)(2,1)S(1)}, f32[1,128]{1,0:T(1,128)S(1)}) custom-call(s32[1]{0:T(128)S(6)} %copy.14.len_ref, bf16[8,72,128]{2,1,0:T(8,128)(2,1)S(1)} %all_to_all.31.attn_ref, bf16[576,1152]{1,0:T(8,128)(2,1)S(1)} %copy-done, bf16[1,128,1152]{2,1,0:T(8,128)(2,1)S(1)} %copy-done.1), custom_call_target="tpu_custom_call" | custom-call | flops 339738624 | bytes 3000000 | tf_op jit(solution)/shard_map/pallas_call | solution.py:379
  46.7 0.1 shard_map.113
  46.7 3.6 %collective-permute-start.1 = (bf16[1448,128]{1,0:T(8,128)(2,1)S(1)}, bf16[1448,128]{1,0:T(8,128)(2,1)S(1)}, u32[]{:S(2)}, u32[]{:S(2)}) collective-permute-start(bf16[1448,128]{1,0:T(8,128)(2,1)S(1)} %get-tuple-element.27.mine_ref), channel_id=1, source_target_pairs={{0,1},{1,0},{2,3},{3,2},{4,5},{5,4},{6,7},{7,6},{8,9},{9,8},{10,11... | collective-permute-start | bytes 1112072 | tf_op jit(solution)/shard_map/ppermute | solution.py:334
  50.3 1.3 %collective-permute-done.1.got_ref = bf16[1448,128]{1,0:T(8,128)(2,1)S(1)} collective-permute-done((bf16[1448,128]{1,0:T(8,128)(2,1)S(1)}, bf16[1448,128]{1,0:T(8,128)(2,1)S(1)}, u32[]{:S(2)}, u32[]{:S(2)}) %collective-permute-start.1) | collective-permute-done | bytes 370720 | tf_op jit(solution)/shard_map/ppermute | solution.py:334
  51.6 0.6 shard_map.114
  52.2 14.8 %all_to_all.32.part_ref = bf16[4,8,88,128]{3,2,1,0:T(8,128)(2,1)S(1)} all-to-all(bf16[4,8,88,128]{3,2,1,0:T(8,128)(2,1)S(1)} %shard_map.114), channel_id=1, replica_groups=mesh['dp_0'=4,'dp_1'=8,'patch_0'=8,'patch_1'=2] {'dp_0'}, dimensions={0} | all-to-all | bytes 1441792 | tf_op jit(solution)/shard_map/all_to_all | solution.py:330
  67.1 3.4 %all-to-all-start.4 = ((bf16[8,72,128]{2,1,0:T(8,128)(2,1)}), bf16[8,72,128]{2,1,0:T(8,128)(2,1)S(1)}, u32[]{:S(2)}, u32[]{:S(2)}) async-start(bf16[8,72,128]{2,1,0:T(8,128)(2,1)} %get-tuple-element.29), calls=%async_computation.4 | async-start | bytes 294912 | tf_op jit(solution)/shard_map/all_to_all | solution.py:330
  70.5 0.8 shard_map.115
  71.3 7.3 %all-to-all-done.4.back_ref = bf16[8,72,128]{2,1,0:T(8,128)(2,1)S(1)} async-done(((bf16[8,72,128]{2,1,0:T(8,128)(2,1)}), bf16[8,72,128]{2,1,0:T(8,128)(2,1)S(1)}, u32[]{:S(2)}, u32[]{:S(2)}) %all-to-all-start.4) | async-done | bytes 147488 | tf_op jit(solution)/shard_map/all_to_all | solution.py:330
  78.6 10.0 %all-to-all-start.3 = ((bf16[8,88,128]{2,1,0:T(8,128)(2,1)}), bf16[8,88,128]{2,1,0:T(8,128)(2,1)S(1)}, u32[]{:S(2)}, u32[]{:S(2)}) async-start(bf16[8,88,128]{2,1,0:T(8,128)(2,1)} %shard_map.115), calls=%async_computation.3 | async-start | bytes 360448 | tf_op jit(solution)/shard_map/all_to_all | solution.py:330
  88.6 5.4 %shard_map.116 = (bf16[8,72,128]{2,1,0:T(8,128)(2,1)S(1)}, bf16[8,144,128]{2,1,0:T(8,128)(2,1)S(1)}, bf16[8,144,128]{2,1,0:T(8,128)(2,1)S(1)}) custom-call(bf16[8,224,128]{2,1,0:T(8,128)(2,1)S(1)} %all_to_all.30.own_ref, bf16[8,224,128]{2,1,0:T(8,128)(2,1)S(1)} %collective-permute-done.other_ref, bf16[8,72,128]{2,1,0:T(8,128)(2,1)S(1)} %get-tuple-element.24.attn_ref, ...), custom_call_target="tpu_custom_call" | custom-call | flops 1207959552 | bytes 6000000 | tf_op jit(solution)/shard_map/pallas_call | solution.py:401
  94.1 4.8 %collective-permute-start.2 = (bf16[8,144,128]{2,1,0:T(8,128)(2,1)S(1)}, bf16[8,144,128]{2,1,0:T(8,128)(2,1)S(1)}, u32[]{:S(2)}, u32[]{:S(2)}) collective-permute-start(bf16[8,144,128]{2,1,0:T(8,128)(2,1)S(1)} %get-tuple-element.35), channel_id=1, source_target_pairs={{0,1},{1,0},{2,3},{3,2},{4,5},{5,4},{6,7},{7,6},{8,9},{9,8},{10,11... | collective-permute-start | bytes 884744 | tf_op jit(solution)/shard_map/ppermute | solution.py:334
  98.8 1.2 collective-permute-done.2.other_ref
  100.0 0.1 shard_map.117.join_ref
  100.1 0.0 all-to-all-done.3.part_ref
  100.1 0.3 shard_map.118
  100.4 17.6 %all_to_all.33.rows_ref = bf16[8,232,128]{2,1,0:T(8,128)(2,1)S(1)} all-to-all(bf16[8,232,128]{2,1,0:T(8,128)(2,1)S(1)} %get-tuple-element.36), channel_id=1, replica_groups=mesh['dp_0'=4,'dp_1'=8,'patch_0'=8,'patch_1'=2] {'patch_0'}, dimensions={0} | all-to-all | bytes 950272 | tf_op jit(solution)/shard_map/all_to_all | solution.py:330
  118.0 0.9 shard_map.119
Async XLA Ops:
  0.6 44.4 %copy-start = (bf16[576,1152]{1,0:T(8,128)(2,1)S(1)}, bf16[576,1152]{1,0:T(8,128)(2,1)}, u32[]{:S(2)}) copy-start(bf16[576,1152]{1,0:T(8,128)(2,1)} %weight_ref.1) | copy-start | bytes 3981316
  0.6 44.4 %copy-start.1 = (bf16[1,128,1152]{2,1,0:T(8,128)(2,1)S(1)}, bf16[1,128,1152]{2,1,0:T(8,128)(2,1)}, u32[]{:S(2)}) copy-start(bf16[1,128,1152]{2,1,0:T(8,128)(2,1)} %target_ref.1) | copy-start | bytes 884740
  23.4 6.3 %collective-permute-start = (bf16[8,224,128]{2,1,0:T(8,128)(2,1)S(1)}, bf16[8,224,128]{2,1,0:T(8,128)(2,1)S(1)}, u32[]{:S(2)}, u32[]{:S(2)}) collective-permute-start(bf16[8,224,128]{2,1,0:T(8,128)(2,1)S(1)} %all_to_all.30.own_ref), channel_id=1, source_target_pairs={{0,1},{1,0},{2,3},{3,2},{4,5},{5,4},{6,7},{7,6},{8,9},{9,8},{10,11... | collective-permute-start | bytes 1376264 | tf_op jit(solution)/shard_map/ppermute | solution.py:334
  46.7 4.9 %collective-permute-start.1 = (bf16[1448,128]{1,0:T(8,128)(2,1)S(1)}, bf16[1448,128]{1,0:T(8,128)(2,1)S(1)}, u32[]{:S(2)}, u32[]{:S(2)}) collective-permute-start(bf16[1448,128]{1,0:T(8,128)(2,1)S(1)} %get-tuple-element.27.mine_ref), channel_id=1, source_target_pairs={{0,1},{1,0},{2,3},{3,2},{4,5},{5,4},{6,7},{7,6},{8,9},{9,8},{10,11... | collective-permute-start | bytes 1112072 | tf_op jit(solution)/shard_map/ppermute | solution.py:334
  67.1 11.5 %all-to-all-start.4 = ((bf16[8,72,128]{2,1,0:T(8,128)(2,1)}), bf16[8,72,128]{2,1,0:T(8,128)(2,1)S(1)}, u32[]{:S(2)}, u32[]{:S(2)}) async-start(bf16[8,72,128]{2,1,0:T(8,128)(2,1)} %get-tuple-element.29), calls=%async_computation.4 | async-start | bytes 294912 | tf_op jit(solution)/shard_map/all_to_all | solution.py:330
  78.6 21.5 %all-to-all-start.3 = ((bf16[8,88,128]{2,1,0:T(8,128)(2,1)}), bf16[8,88,128]{2,1,0:T(8,128)(2,1)S(1)}, u32[]{:S(2)}, u32[]{:S(2)}) async-start(bf16[8,88,128]{2,1,0:T(8,128)(2,1)} %shard_map.115), calls=%async_computation.3 | async-start | bytes 360448 | tf_op jit(solution)/shard_map/all_to_all | solution.py:330
  94.1 5.9 %collective-permute-start.2 = (bf16[8,144,128]{2,1,0:T(8,128)(2,1)S(1)}, bf16[8,144,128]{2,1,0:T(8,128)(2,1)S(1)}, u32[]{:S(2)}, u32[]{:S(2)}) collective-permute-start(bf16[8,144,128]{2,1,0:T(8,128)(2,1)S(1)} %get-tuple-element.35), channel_id=1, source_target_pairs={{0,1},{1,0},{2,3},{3,2},{4,5},{5,4},{6,7},{7,6},{8,9},{9,8},{10,11... | collective-permute-start | bytes 884744 | tf_op jit(solution)/shard_map/ppermute | solution.py:334

commit v4 on v3

--- a/solution.py
+++ b/solution.py
@@ -25,7 +25,6 @@
 PAD = 88
 THIRD = ROWS // 3
 LAST = 16
-DEPTH = 8
 PAIR = WIDTH + HALF + 8
 BUF = 3 * HD + 8
 QB = 256
@@ -208,17 +207,7 @@
             jnp.concatenate(rest, axis=1),
             tail,
         ]
-        out_ref[d // DEPTH, d % DEPTH] = jnp.concatenate(block, axis=0).astype(BF16)
-
-
-def sum_kernel(part_ref, out_ref):
-    total = part_ref[0].astype(F32)
-    for x in range(1, SAMPLES // DEPTH):
-        total = total + part_ref[x].astype(F32)
-    out_ref[...] = total.astype(BF16)
-    tail = stat_rows(*stats_of(total[0])).astype(BF16)
-    for z in range(DEPTH):
-        out_ref[z, STAT:PAD, :] = tail
+        out_ref[d] = jnp.concatenate(block, axis=0).astype(BF16)
 
 
 def backward_kernel(
@@ -287,7 +276,7 @@
 def reduce_kernel(part_ref, join_ref, out_ref, stat_ref, last_sc, sem):
     del join_ref
     total = part_ref[0].astype(F32)
-    for d in range(1, DEPTH):
+    for d in range(1, SAMPLES):
         total = total + part_ref[d].astype(F32)
     count, loss = stats_of(total)
     stat_ref[...] = jnp.broadcast_to(count, (8, TOK))
@@ -390,13 +379,13 @@
     got_pair = swap(mine)
     weight_part = call(
         weight_kernel,
-        shape((SAMPLES // DEPTH, DEPTH, PAD, TOK), BF16),
+        shape((SAMPLES, PAD, TOK), BF16),
         [SM, VM, VM, VM],
         2 * TOK * FEAT * WIDTH,
         3 * 10**6,
         [pltpu.VMEM((WIDTH, 3 * TOK), F32)],
     )(lengths, mine, got_pair, half)
-    weight_rows = exchange(weight_part, "dp_0")
+    weight_parts = exchange(weight_part, DP)
     pair = shape((CHIPS, 2 * HD, TOK), BF16)
     query_grad, own_grad, other_grad = call(
         backward_kernel,
@@ -414,8 +403,6 @@
         ],
         24,
     )(own, other, attn, back_heads, near, in_hbm(far), inv)
-    weight_row = call(sum_kernel, shape((DEPTH, PAD, TOK), BF16), [VM], 10**6, 10**6)(weight_rows)
-    weight_parts = exchange(weight_row, "dp_1")
     got = swap(other_grad)
     both = shape((CHIPS, 3 * HD + LAST, TOK), BF16)
     joined = call(join_kernel, both, [VM] * 3, 10**6, 10**6)(query_grad, own_grad, got)

time: 120 us -> 116 us (0.967)
  the two profiles are of different devices: /device:TPU:1 before, /device:TPU:64 now
where the time goes in v4:
time: 116 us
  blocking collectives  52.5 us (45%)
  waiting for transfers between devices  24.4 us (21%)
  starting transfers between devices  21.7 us (19%)
  Pallas kernels  15.5 us (13%)
  between operations  1.39 us (1%)
    all_to_all x3, blocking collectives, exchange(): return lax.all_to_all(value, axis, 0, 0, tiled=True)  52.5 us
    all_to_all x2, waiting for transfers between devices, exchange(): return lax.all_to_all(value, axis, 0, 0, tiled=True)  21.7 us
    all_to_all x2, starting transfers between devices, exchange(): return lax.all_to_all(value, axis, 0, 0, tiled=True)  16 us
    ppermute x3, starting transfers between devices, swap(): return lax.ppermute(value, 'patch_1', [(0, 1), (1, 0)])  5.75 us
    pallas_call x1, Pallas kernels, local(): call(backward_kernel, (heads, pair, pair), [VM, VM, VM, VM, VM, HB, VM],...  5.44 us
    pallas_call x1, Pallas kernels, local(): call(forward_kernel, (heads, shape((NEAR, SEQ, QB), BF16), pltpu.HBM((FAR...  4.27 us
    ppermute x3, waiting for transfers between devices, swap(): return lax.ppermute(value, 'patch_1', [(0, 1), (1, 0)])  2.69 us
  transfers between devices with their start and end apart: 5, of which 4 were waited for; matrix products, arithmetic and copies ran while one was open for 0% of the time, Pallas kernels for 6%

profile of v4, /device:TPU:64, one launch (start us, length us, event | category | flops | bytes accessed | tf_op | source)
XLA Modules:
  0.0 115.5 jit_solution(13572359878251557597)
XLA Ops:
  0.6 0.0 copy-start
  0.6 0.0 copy-start.1
  0.7 1.2 %shard_map.110 = bf16[8,224,128]{2,1,0:T(8,128)(2,1)S(1)} custom-call(bf16[8,72,128]{2,1,0:T(8,128)(2,1)} %bitcast.13, bf16[8,72,128]{2,1,0:T(8,128)(2,1)} %bitcast.14, bf16[8,72,128]{2,1,0:T(8,128)(2,1)} %bitcast.15, s32[1,128]{1,0:T(1,128)} %seg_ref.1), custom_call_target="tpu_custom_call" | custom-call | flops 1000000 | bytes 1000000 | tf_op jit(solution)/shard_map/pallas_call | solution.py:337
  1.9 23.0 %all_to_all.25.own_ref = bf16[8,224,128]{2,1,0:T(8,128)(2,1)S(1)} all-to-all(bf16[8,224,128]{2,1,0:T(8,128)(2,1)S(1)} %shard_map.110), channel_id=1, replica_groups=mesh['dp_0'=4,'dp_1'=8,'patch_0'=8,'patch_1'=2] {'patch_0'}, dimensions={0} | all-to-all | bytes 917504 | tf_op jit(solution)/shard_map/all_to_all | solution.py:319
  24.9 1.9 %collective-permute-start = (bf16[8,224,128]{2,1,0:T(8,128)(2,1)S(1)}, bf16[8,224,128]{2,1,0:T(8,128)(2,1)S(1)}, u32[]{:S(2)}, u32[]{:S(2)}) collective-permute-start(bf16[8,224,128]{2,1,0:T(8,128)(2,1)S(1)} %all_to_all.25.own_ref), channel_id=1, source_target_pairs={{0,1},{1,0},{2,3},{3,2},{4,5},{5,4},{6,7},{7,6},{8,9},{9,8},{10,11... | collective-permute-start | bytes 1376264 | tf_op jit(solution)/shard_map/ppermute | solution.py:323
  27.4 1.1 collective-permute-done.other_ref
  28.6 4.3 %shard_map.111 = (bf16[8,72,128]{2,1,0:T(8,128)(2,1)S(1)}, bf16[1,2048,256]{2,1,0:T(8,128)(2,1)S(1)}, bf16[3,2048,256]{2,1,0:T(8,128)(2,1)}, f32[4,256]{1,0:T(4,128)S(1)}) custom-call(s32[1]{0:T(128)S(6)} %copy.14.len_ref, bf16[8,224,128]{2,1,0:T(8,128)(2,1)S(1)} %all_to_all.25.own_ref, bf16[8,224,128]{2,1,0:T(8,128)(2,1)S(1)} %collective-permute-done.other_ref), custom_call_target="tpu_custom_call" | custom-call | flops 603979776 | bytes 6000000 | tf_op jit(solution)/shard_map/pallas_call | solution.py:349
  32.8 12.4 %all_to_all.26.attn_ref = bf16[8,72,128]{2,1,0:T(8,128)(2,1)S(1)} all-to-all(bf16[8,72,128]{2,1,0:T(8,128)(2,1)S(1)} %get-tuple-element.24.attn_ref), channel_id=1, replica_groups=mesh['dp_0'=4,'dp_1'=8,'patch_0'=8,'patch_1'=2] {'patch_0'}, dimensions={0} | all-to-all | bytes 294912 | tf_op jit(solution)/shard_map/all_to_all | solution.py:319
  45.2 0.0 copy-done
  45.2 0.0 copy-done.1
  45.2 1.7 %shard_map.112 = (bf16[8,72,128]{2,1,0:T(8,128)(2,1)}, bf16[1152,128]{1,0:T(8,128)(2,1)S(1)}, f32[1,128]{1,0:T(1,128)S(1)}) custom-call(s32[1]{0:T(128)S(6)} %copy.14.len_ref, bf16[8,72,128]{2,1,0:T(8,128)(2,1)S(1)} %all_to_all.26.attn_ref, bf16[576,1152]{1,0:T(8,128)(2,1)S(1)} %copy-done, bf16[1,128,1152]{2,1,0:T(8,128)(2,1)S(1)} %copy-done.1), custom_call_target="tpu_custom_call" | custom-call | flops 339738624 | bytes 3000000 | tf_op jit(solution)/shard_map/pallas_call | solution.py:368
  46.9 0.1 shard_map.113
  46.9 1.9 %collective-permute-start.1 = (bf16[1448,128]{1,0:T(8,128)(2,1)S(1)}, bf16[1448,128]{1,0:T(8,128)(2,1)S(1)}, u32[]{:S(2)}, u32[]{:S(2)}) collective-permute-start(bf16[1448,128]{1,0:T(8,128)(2,1)S(1)} %get-tuple-element.27.mine_ref), channel_id=1, source_target_pairs={{0,1},{1,0},{2,3},{3,2},{4,5},{5,4},{6,7},{7,6},{8,9},{9,8},{10,11... | collective-permute-start | bytes 1112072 | tf_op jit(solution)/shard_map/ppermute | solution.py:323
  48.9 3.4 %all-to-all-start.3 = ((bf16[8,72,128]{2,1,0:T(8,128)(2,1)}), bf16[8,72,128]{2,1,0:T(8,128)(2,1)S(1)}, u32[]{:S(2)}, u32[]{:S(2)}) async-start(bf16[8,72,128]{2,1,0:T(8,128)(2,1)} %get-tuple-element.29), calls=%async_computation.3 | async-start | bytes 294912 | tf_op jit(solution)/shard_map/all_to_all | solution.py:319
  52.3 0.0 collective-permute-done.1.got_ref
  52.3 1.5 %shard_map.114 = bf16[32,88,128]{2,1,0:T(8,128)(2,1)} custom-call(s32[1]{0:T(128)S(6)} %copy.14.len_ref, bf16[1448,128]{1,0:T(8,128)(2,1)S(1)} %get-tuple-element.27.mine_ref, bf16[1448,128]{1,0:T(8,128)(2,1)S(1)} %collective-permute-done.1.got_ref, bf16[288,128]{1,0:T(8,128)(2,1)S(1)} %get-tuple-element.28.half_ref), custom_call_target="tpu_custom_call" | custom-call | flops 169869312 | bytes 3000000 | tf_op jit(solution)/shard_map/pallas_call | solution.py:380
  53.7 8.8 %all-to-all-done.3.back_ref = bf16[8,72,128]{2,1,0:T(8,128)(2,1)S(1)} async-done(((bf16[8,72,128]{2,1,0:T(8,128)(2,1)}), bf16[8,72,128]{2,1,0:T(8,128)(2,1)S(1)}, u32[]{:S(2)}, u32[]{:S(2)}) %all-to-all-start.3) | async-done | bytes 147488 | tf_op jit(solution)/shard_map/all_to_all | solution.py:319
  62.5 12.6 %all-to-all-start.2 = ((bf16[32,88,128]{2,1,0:T(8,128)(2,1)}), bf16[32,88,128]{2,1,0:T(8,128)(2,1)S(1)}, u32[]{:S(2)}, u32[]{:S(2)}) async-start(bf16[32,88,128]{2,1,0:T(8,128)(2,1)} %shard_map.114), calls=%async_computation.2 | async-start | bytes 1441792 | tf_op jit(solution)/shard_map/all_to_all | solution.py:319
  75.1 5.4 %shard_map.115 = (bf16[8,72,128]{2,1,0:T(8,128)(2,1)S(1)}, bf16[8,144,128]{2,1,0:T(8,128)(2,1)S(1)}, bf16[8,144,128]{2,1,0:T(8,128)(2,1)S(1)}) custom-call(bf16[8,224,128]{2,1,0:T(8,128)(2,1)S(1)} %all_to_all.25.own_ref, bf16[8,224,128]{2,1,0:T(8,128)(2,1)S(1)} %collective-permute-done.other_ref, bf16[8,72,128]{2,1,0:T(8,128)(2,1)S(1)} %get-tuple-element.24.attn_ref, ...), custom_call_target="tpu_custom_call" | custom-call | flops 1207959552 | bytes 6000000 | tf_op jit(solution)/shard_map/pallas_call | solution.py:390
  80.6 1.9 %collective-permute-start.2 = (bf16[8,144,128]{2,1,0:T(8,128)(2,1)S(1)}, bf16[8,144,128]{2,1,0:T(8,128)(2,1)S(1)}, u32[]{:S(2)}, u32[]{:S(2)}) collective-permute-start(bf16[8,144,128]{2,1,0:T(8,128)(2,1)S(1)} %get-tuple-element.35), channel_id=1, source_target_pairs={{0,1},{1,0},{2,3},{3,2},{4,5},{5,4},{6,7},{7,6},{8,9},{9,8},{10,11... | collective-permute-start | bytes 884744 | tf_op jit(solution)/shard_map/ppermute | solution.py:323
  82.5 1.5 %collective-permute-done.2.other_ref = bf16[8,144,128]{2,1,0:T(8,128)(2,1)S(1)} collective-permute-done((bf16[8,144,128]{2,1,0:T(8,128)(2,1)S(1)}, bf16[8,144,128]{2,1,0:T(8,128)(2,1)S(1)}, u32[]{:S(2)}, u32[]{:S(2)}) %collective-permute-start.2) | collective-permute-done | bytes 294944 | tf_op jit(solution)/shard_map/ppermute | solution.py:323
  84.0 0.1 shard_map.116.join_ref
  84.1 12.9 %all-to-all-done.2.part_ref = bf16[32,88,128]{2,1,0:T(8,128)(2,1)S(1)} async-done(((bf16[32,88,128]{2,1,0:T(8,128)(2,1)}), bf16[32,88,128]{2,1,0:T(8,128)(2,1)S(1)}, u32[]{:S(2)}, u32[]{:S(2)}) %all-to-all-start.2) | async-done | bytes 720928 | tf_op jit(solution)/shard_map/all_to_all | solution.py:319
  97.1 0.4 shard_map.117
  97.5 17.1 %all_to_all.27.rows_ref = bf16[8,232,128]{2,1,0:T(8,128)(2,1)S(1)} all-to-all(bf16[8,232,128]{2,1,0:T(8,128)(2,1)S(1)} %get-tuple-element.36), channel_id=1, replica_groups=mesh['dp_0'=4,'dp_1'=8,'patch_0'=8,'patch_1'=2] {'patch_0'}, dimensions={0} | all-to-all | bytes 950272 | tf_op jit(solution)/shard_map/all_to_all | solution.py:319
  114.6 0.9 shard_map.118
Async XLA Ops:
  0.6 44.6 %copy-start = (bf16[576,1152]{1,0:T(8,128)(2,1)S(1)}, bf16[576,1152]{1,0:T(8,128)(2,1)}, u32[]{:S(2)}) copy-start(bf16[576,1152]{1,0:T(8,128)(2,1)} %weight_ref.1) | copy-start | bytes 3981316
  0.6 44.6 %copy-start.1 = (bf16[1,128,1152]{2,1,0:T(8,128)(2,1)S(1)}, bf16[1,128,1152]{2,1,0:T(8,128)(2,1)}, u32[]{:S(2)}) copy-start(bf16[1,128,1152]{2,1,0:T(8,128)(2,1)} %target_ref.1) | copy-start | bytes 884740
  24.9 3.7 %collective-permute-start = (bf16[8,224,128]{2,1,0:T(8,128)(2,1)S(1)}, bf16[8,224,128]{2,1,0:T(8,128)(2,1)S(1)}, u32[]{:S(2)}, u32[]{:S(2)}) collective-permute-start(bf16[8,224,128]{2,1,0:T(8,128)(2,1)S(1)} %all_to_all.25.own_ref), channel_id=1, source_target_pairs={{0,1},{1,0},{2,3},{3,2},{4,5},{5,4},{6,7},{7,6},{8,9},{9,8},{10,11... | collective-permute-start | bytes 1376264 | tf_op jit(solution)/shard_map/ppermute | solution.py:323
  46.9 5.3 %collective-permute-start.1 = (bf16[1448,128]{1,0:T(8,128)(2,1)S(1)}, bf16[1448,128]{1,0:T(8,128)(2,1)S(1)}, u32[]{:S(2)}, u32[]{:S(2)}) collective-permute-start(bf16[1448,128]{1,0:T(8,128)(2,1)S(1)} %get-tuple-element.27.mine_ref), channel_id=1, source_target_pairs={{0,1},{1,0},{2,3},{3,2},{4,5},{5,4},{6,7},{7,6},{8,9},{9,8},{10,11... | collective-permute-start | bytes 1112072 | tf_op jit(solution)/shard_map/ppermute | solution.py:323
  48.9 13.7 %all-to-all-start.3 = ((bf16[8,72,128]{2,1,0:T(8,128)(2,1)}), bf16[8,72,128]{2,1,0:T(8,128)(2,1)S(1)}, u32[]{:S(2)}, u32[]{:S(2)}) async-start(bf16[8,72,128]{2,1,0:T(8,128)(2,1)} %get-tuple-element.29), calls=%async_computation.3 | async-start | bytes 294912 | tf_op jit(solution)/shard_map/all_to_all | solution.py:319
  62.5 34.5 %all-to-all-start.2 = ((bf16[32,88,128]{2,1,0:T(8,128)(2,1)}), bf16[32,88,128]{2,1,0:T(8,128)(2,1)S(1)}, u32[]{:S(2)}, u32[]{:S(2)}) async-start(bf16[32,88,128]{2,1,0:T(8,128)(2,1)} %shard_map.114), calls=%async_computation.2 | async-start | bytes 1441792 | tf_op jit(solution)/shard_map/all_to_all | solution.py:319
  80.6 3.5 %collective-permute-start.2 = (bf16[8,144,128]{2,1,0:T(8,128)(2,1)S(1)}, bf16[8,144,128]{2,1,0:T(8,128)(2,1)S(1)}, u32[]{:S(2)}, u32[]{:S(2)}) collective-permute-start(bf16[8,144,128]{2,1,0:T(8,128)(2,1)S(1)} %get-tuple-element.35), channel_id=1, source_target_pairs={{0,1},{1,0},{2,3},{3,2},{4,5},{5,4},{6,7},{7,6},{8,9},{9,8},{10,11... | collective-permute-start | bytes 884744 | tf_op jit(solution)/shard_map/ppermute | solution.py:323

commit v5 on v4

--- a/solution.py
+++ b/solution.py
@@ -296,19 +296,26 @@
     copy.wait()
 
 
-def unpack_kernel(rows_ref, stat_ref, query_ref, key_ref, value_ref, weight_ref, loss_ref):
+def unpack_kernel(
+    rows_ref, stat_ref, query_ref, key_ref, value_ref, weight_ref, loss_ref, grad_sc, sems
+):
+    copies = []
     count = stat_ref[0:1, :]
     ratio = float(SAMPLES * SEQ) / count
     for at, (ref, factor) in enumerate(((query_ref, SCALE), (key_ref, SCALE), (value_ref, 1.0))):
         for h in range(HEADS):
             rows = rows_ref[h, at * HD : (at + 1) * HD, :].astype(F32)
-            ref[0, h * HD : (h + 1) * HD, :] = rows * (ratio * factor)
+            grad_sc[at, h * HD : (h + 1) * HD, :] = rows * (ratio * factor)
+        copies.append(pltpu.make_async_copy(grad_sc.at[at], ref.at[0], sems.at[at]))
+        copies[at].start()
     total = sum(rows_ref[c, 3 * HD : 3 * HD + LAST, :].astype(F32) for c in range(CHIPS))
     scaled = total * (ratio / SEQ)
     thirds = [scaled[0:THIRD, i * COLS : (i + 1) * COLS] for i in range(3)]
     weight_ref[...] = jnp.concatenate(thirds, axis=0)
     loss = jnp.sum(total[THIRD : THIRD + 1] + total[THIRD + 1 : THIRD + 2], axis=1, keepdims=True)
     loss_ref[...] = loss / (count[:, 0:1] * WIDTH)
+    for copy in copies:
+        copy.wait()
 
 
 def in_hbm(value):
@@ -417,13 +424,15 @@
         aliases={1: 0},
     )(weight_parts, joined)
     grads = exchange(joined, "patch_0")
-    rows = shape((1, FEAT, TOK), F32)
+    rows = pltpu.HBM((1, FEAT, TOK), F32)
     query_out, key_out, value_out, weight_grad, loss = call(
         unpack_kernel,
         (rows, rows, rows, shape((ROWS, COLS), F32), shape((1, 1), F32)),
         [VM, VM],
         10**6,
         10**6,
+        [pltpu.VMEM((3, FEAT, TOK), F32), pltpu.SemaphoreType.DMA((3,))],
+        outs=(HB, HB, HB, VM, VM),
     )(grads, stats)
     grads_out = (jnp.swapaxes(rows, 1, 2) for rows in (query_out, key_out, value_out))
     return *grads_out, weight_grad, loss[0, 0]

time: 116 us -> 117 us (level)
  no operation moved by 1% of the time
where the time goes in v5:
time: 117 us; the launch traced here: 116 us
  blocking collectives  52.5 us (45%)
  waiting for transfers between devices  24.4 us (21%)
  starting transfers between devices  21.7 us (19%)
  Pallas kernels  16.2 us (14%)
  between operations  1.39 us (1%)
    all_to_all x3, blocking collectives, exchange(): return lax.all_to_all(value, axis, 0, 0, tiled=True)  52.5 us
    all_to_all x2, waiting for transfers between devices, exchange(): return lax.all_to_all(value, axis, 0, 0, tiled=True)  21.7 us
    all_to_all x2, starting transfers between devices, exchange(): return lax.all_to_all(value, axis, 0, 0, tiled=True)  16 us
    ppermute x3, starting transfers between devices, swap(): return lax.ppermute(value, 'patch_1', [(0, 1), (1, 0)])  5.75 us
    pallas_call x1, Pallas kernels, local(): call(backward_kernel, (heads, pair, pair), [VM, VM, VM, VM, VM, HB, VM],...  5.44 us
    pallas_call x1, Pallas kernels, local(): call(forward_kernel, (heads, shape((NEAR, SEQ, QB), BF16), pltpu.HBM((FAR...  4.27 us
    ppermute x3, waiting for transfers between devices, swap(): return lax.ppermute(value, 'patch_1', [(0, 1), (1, 0)])  2.69 us
  transfers between devices with their start and end apart: 5, of which 4 were waited for; matrix products, arithmetic and copies ran while one was open for 0% of the time, Pallas kernels for 6%

profile of v5, /device:TPU:64, one launch (start us, length us, event | category | flops | bytes accessed | tf_op | source)
XLA Modules:
  0.0 116.1 jit_solution(17511755474109079405)
XLA Ops:
  0.6 0.0 copy-start
  0.6 0.0 copy-start.1
  0.7 1.2 %shard_map.110 = bf16[8,224,128]{2,1,0:T(8,128)(2,1)S(1)} custom-call(bf16[8,72,128]{2,1,0:T(8,128)(2,1)} %bitcast.13, bf16[8,72,128]{2,1,0:T(8,128)(2,1)} %bitcast.14, bf16[8,72,128]{2,1,0:T(8,128)(2,1)} %bitcast.15, s32[1,128]{1,0:T(1,128)} %seg_ref.1), custom_call_target="tpu_custom_call" | custom-call | flops 1000000 | bytes 1000000 | tf_op jit(solution)/shard_map/pallas_call | solution.py:344
  1.9 23.0 %all_to_all.25.own_ref = bf16[8,224,128]{2,1,0:T(8,128)(2,1)S(1)} all-to-all(bf16[8,224,128]{2,1,0:T(8,128)(2,1)S(1)} %shard_map.110), channel_id=1, replica_groups=mesh['dp_0'=4,'dp_1'=8,'patch_0'=8,'patch_1'=2] {'patch_0'}, dimensions={0} | all-to-all | bytes 917504 | tf_op jit(solution)/shard_map/all_to_all | solution.py:326
  24.9 1.9 %collective-permute-start = (bf16[8,224,128]{2,1,0:T(8,128)(2,1)S(1)}, bf16[8,224,128]{2,1,0:T(8,128)(2,1)S(1)}, u32[]{:S(2)}, u32[]{:S(2)}) collective-permute-start(bf16[8,224,128]{2,1,0:T(8,128)(2,1)S(1)} %all_to_all.25.own_ref), channel_id=1, source_target_pairs={{0,1},{1,0},{2,3},{3,2},{4,5},{5,4},{6,7},{7,6},{8,9},{9,8},{10,11... | collective-permute-start | bytes 1376264 | tf_op jit(solution)/shard_map/ppermute | solution.py:330
  27.4 1.1 collective-permute-done.other_ref
  28.6 4.3 %shard_map.111 = (bf16[8,72,128]{2,1,0:T(8,128)(2,1)S(1)}, bf16[1,2048,256]{2,1,0:T(8,128)(2,1)S(1)}, bf16[3,2048,256]{2,1,0:T(8,128)(2,1)}, f32[4,256]{1,0:T(4,128)S(1)}) custom-call(s32[1]{0:T(128)S(6)} %copy.14.len_ref, bf16[8,224,128]{2,1,0:T(8,128)(2,1)S(1)} %all_to_all.25.own_ref, bf16[8,224,128]{2,1,0:T(8,128)(2,1)S(1)} %collective-permute-done.other_ref), custom_call_target="tpu_custom_call" | custom-call | flops 603979776 | bytes 6000000 | tf_op jit(solution)/shard_map/pallas_call | solution.py:356
  32.8 12.4 %all_to_all.26.attn_ref = bf16[8,72,128]{2,1,0:T(8,128)(2,1)S(1)} all-to-all(bf16[8,72,128]{2,1,0:T(8,128)(2,1)S(1)} %get-tuple-element.24.attn_ref), channel_id=1, replica_groups=mesh['dp_0'=4,'dp_1'=8,'patch_0'=8,'patch_1'=2] {'patch_0'}, dimensions={0} | all-to-all | bytes 294912 | tf_op jit(solution)/shard_map/all_to_all | solution.py:326
  45.2 0.0 copy-done
  45.2 0.0 copy-done.1
  45.2 1.7 %shard_map.112 = (bf16[8,72,128]{2,1,0:T(8,128)(2,1)}, bf16[1152,128]{1,0:T(8,128)(2,1)S(1)}, f32[1,128]{1,0:T(1,128)S(1)}) custom-call(s32[1]{0:T(128)S(6)} %copy.14.len_ref, bf16[8,72,128]{2,1,0:T(8,128)(2,1)S(1)} %all_to_all.26.attn_ref, bf16[576,1152]{1,0:T(8,128)(2,1)S(1)} %copy-done, bf16[1,128,1152]{2,1,0:T(8,128)(2,1)S(1)} %copy-done.1), custom_call_target="tpu_custom_call" | custom-call | flops 339738624 | bytes 3000000 | tf_op jit(solution)/shard_map/pallas_call | solution.py:375
  46.9 0.1 shard_map.113
  46.9 1.9 %collective-permute-start.1 = (bf16[1448,128]{1,0:T(8,128)(2,1)S(1)}, bf16[1448,128]{1,0:T(8,128)(2,1)S(1)}, u32[]{:S(2)}, u32[]{:S(2)}) collective-permute-start(bf16[1448,128]{1,0:T(8,128)(2,1)S(1)} %get-tuple-element.27.mine_ref), channel_id=1, source_target_pairs={{0,1},{1,0},{2,3},{3,2},{4,5},{5,4},{6,7},{7,6},{8,9},{9,8},{10,11... | collective-permute-start | bytes 1112072 | tf_op jit(solution)/shard_map/ppermute | solution.py:330
  48.9 3.4 %all-to-all-start.3 = ((bf16[8,72,128]{2,1,0:T(8,128)(2,1)}), bf16[8,72,128]{2,1,0:T(8,128)(2,1)S(1)}, u32[]{:S(2)}, u32[]{:S(2)}) async-start(bf16[8,72,128]{2,1,0:T(8,128)(2,1)} %get-tuple-element.29), calls=%async_computation.3 | async-start | bytes 294912 | tf_op jit(solution)/shard_map/all_to_all | solution.py:326
  52.3 0.0 collective-permute-done.1.got_ref
  52.3 1.5 %shard_map.114 = bf16[32,88,128]{2,1,0:T(8,128)(2,1)} custom-call(s32[1]{0:T(128)S(6)} %copy.14.len_ref, bf16[1448,128]{1,0:T(8,128)(2,1)S(1)} %get-tuple-element.27.mine_ref, bf16[1448,128]{1,0:T(8,128)(2,1)S(1)} %collective-permute-done.1.got_ref, bf16[288,128]{1,0:T(8,128)(2,1)S(1)} %get-tuple-element.28.half_ref), custom_call_target="tpu_custom_call" | custom-call | flops 169869312 | bytes 3000000 | tf_op jit(solution)/shard_map/pallas_call | solution.py:387
  53.7 8.8 %all-to-all-done.3.back_ref = bf16[8,72,128]{2,1,0:T(8,128)(2,1)S(1)} async-done(((bf16[8,72,128]{2,1,0:T(8,128)(2,1)}), bf16[8,72,128]{2,1,0:T(8,128)(2,1)S(1)}, u32[]{:S(2)}, u32[]{:S(2)}) %all-to-all-start.3) | async-done | bytes 147488 | tf_op jit(solution)/shard_map/all_to_all | solution.py:326
  62.5 12.6 %all-to-all-start.2 = ((bf16[32,88,128]{2,1,0:T(8,128)(2,1)}), bf16[32,88,128]{2,1,0:T(8,128)(2,1)S(1)}, u32[]{:S(2)}, u32[]{:S(2)}) async-start(bf16[32,88,128]{2,1,0:T(8,128)(2,1)} %shard_map.114), calls=%async_computation.2 | async-start | bytes 1441792 | tf_op jit(solution)/shard_map/all_to_all | solution.py:326
  75.1 5.4 %shard_map.115 = (bf16[8,72,128]{2,1,0:T(8,128)(2,1)S(1)}, bf16[8,144,128]{2,1,0:T(8,128)(2,1)S(1)}, bf16[8,144,128]{2,1,0:T(8,128)(2,1)S(1)}) custom-call(bf16[8,224,128]{2,1,0:T(8,128)(2,1)S(1)} %all_to_all.25.own_ref, bf16[8,224,128]{2,1,0:T(8,128)(2,1)S(1)} %collective-permute-done.other_ref, bf16[8,72,128]{2,1,0:T(8,128)(2,1)S(1)} %get-tuple-element.24.attn_ref, ...), custom_call_target="tpu_custom_call" | custom-call | flops 1207959552 | bytes 6000000 | tf_op jit(solution)/shard_map/pallas_call | solution.py:397
  80.6 1.9 %collective-permute-start.2 = (bf16[8,144,128]{2,1,0:T(8,128)(2,1)S(1)}, bf16[8,144,128]{2,1,0:T(8,128)(2,1)S(1)}, u32[]{:S(2)}, u32[]{:S(2)}) collective-permute-start(bf16[8,144,128]{2,1,0:T(8,128)(2,1)S(1)} %get-tuple-element.35), channel_id=1, source_target_pairs={{0,1},{1,0},{2,3},{3,2},{4,5},{5,4},{6,7},{7,6},{8,9},{9,8},{10,11... | collective-permute-start | bytes 884744 | tf_op jit(solution)/shard_map/ppermute | solution.py:330
  82.5 1.5 %collective-permute-done.2.other_ref = bf16[8,144,128]{2,1,0:T(8,128)(2,1)S(1)} collective-permute-done((bf16[8,144,128]{2,1,0:T(8,128)(2,1)S(1)}, bf16[8,144,128]{2,1,0:T(8,128)(2,1)S(1)}, u32[]{:S(2)}, u32[]{:S(2)}) %collective-permute-start.2) | collective-permute-done | bytes 294944 | tf_op jit(solution)/shard_map/ppermute | solution.py:330
  84.0 0.1 shard_map.116.join_ref
  84.1 12.9 %all-to-all-done.2.part_ref = bf16[32,88,128]{2,1,0:T(8,128)(2,1)S(1)} async-done(((bf16[32,88,128]{2,1,0:T(8,128)(2,1)}), bf16[32,88,128]{2,1,0:T(8,128)(2,1)S(1)}, u32[]{:S(2)}, u32[]{:S(2)}) %all-to-all-start.2) | async-done | bytes 720928 | tf_op jit(solution)/shard_map/all_to_all | solution.py:326
  97.1 0.4 shard_map.117
  97.5 17.1 %all_to_all.27.rows_ref = bf16[8,232,128]{2,1,0:T(8,128)(2,1)S(1)} all-to-all(bf16[8,232,128]{2,1,0:T(8,128)(2,1)S(1)} %get-tuple-element.36), channel_id=1, replica_groups=mesh['dp_0'=4,'dp_1'=8,'patch_0'=8,'patch_1'=2] {'patch_0'}, dimensions={0} | all-to-all | bytes 950272 | tf_op jit(solution)/shard_map/all_to_all | solution.py:326
  114.6 1.6 %shard_map.118 = (f32[1,576,128]{2,1,0:T(8,128)}, f32[1,576,128]{2,1,0:T(8,128)}, f32[1,576,128]{2,1,0:T(8,128)}, f32[36,36]{1,0:T(8,128)}, f32[1,1]{1,0:T(1,128)}) custom-call(bf16[8,232,128]{2,1,0:T(8,128)(2,1)S(1)} %all_to_all.27.rows_ref, f32[8,128]{1,0:T(8,128)S(1)} %get-tuple-element.37.stat_ref), custom_call_target="tpu_custom_call" | custom-call | flops 1000000 | bytes 1000000 | tf_op jit(solution)/shard_map/pallas_call | solution.py:428
Async XLA Ops:
  0.6 44.6 %copy-start = (bf16[576,1152]{1,0:T(8,128)(2,1)S(1)}, bf16[576,1152]{1,0:T(8,128)(2,1)}, u32[]{:S(2)}) copy-start(bf16[576,1152]{1,0:T(8,128)(2,1)} %weight_ref.1) | copy-start | bytes 3981316
  0.6 44.6 %copy-start.1 = (bf16[1,128,1152]{2,1,0:T(8,128)(2,1)S(1)}, bf16[1,128,1152]{2,1,0:T(8,128)(2,1)}, u32[]{:S(2)}) copy-start(bf16[1,128,1152]{2,1,0:T(8,128)(2,1)} %target_ref.1) | copy-start | bytes 884740
  24.9 3.7 %collective-permute-start = (bf16[8,224,128]{2,1,0:T(8,128)(2,1)S(1)}, bf16[8,224,128]{2,1,0:T(8,128)(2,1)S(1)}, u32[]{:S(2)}, u32[]{:S(2)}) collective-permute-start(bf16[8,224,128]{2,1,0:T(8,128)(2,1)S(1)} %all_to_all.25.own_ref), channel_id=1, source_target_pairs={{0,1},{1,0},{2,3},{3,2},{4,5},{5,4},{6,7},{7,6},{8,9},{9,8},{10,11... | collective-permute-start | bytes 1376264 | tf_op jit(solution)/shard_map/ppermute | solution.py:330
  46.9 5.3 %collective-permute-start.1 = (bf16[1448,128]{1,0:T(8,128)(2,1)S(1)}, bf16[1448,128]{1,0:T(8,128)(2,1)S(1)}, u32[]{:S(2)}, u32[]{:S(2)}) collective-permute-start(bf16[1448,128]{1,0:T(8,128)(2,1)S(1)} %get-tuple-element.27.mine_ref), channel_id=1, source_target_pairs={{0,1},{1,0},{2,3},{3,2},{4,5},{5,4},{6,7},{7,6},{8,9},{9,8},{10,11... | collective-permute-start | bytes 1112072 | tf_op jit(solution)/shard_map/ppermute | solution.py:330
  48.9 13.7 %all-to-all-start.3 = ((bf16[8,72,128]{2,1,0:T(8,128)(2,1)}), bf16[8,72,128]{2,1,0:T(8,128)(2,1)S(1)}, u32[]{:S(2)}, u32[]{:S(2)}) async-start(bf16[8,72,128]{2,1,0:T(8,128)(2,1)} %get-tuple-element.29), calls=%async_computation.3 | async-start | bytes 294912 | tf_op jit(solution)/shard_map/all_to_all | solution.py:326
  62.5 34.5 %all-to-all-start.2 = ((bf16[32,88,128]{2,1,0:T(8,128)(2,1)}), bf16[32,88,128]{2,1,0:T(8,128)(2,1)S(1)}, u32[]{:S(2)}, u32[]{:S(2)}) async-start(bf16[32,88,128]{2,1,0:T(8,128)(2,1)} %shard_map.114), calls=%async_computation.2 | async-start | bytes 1441792 | tf_op jit(solution)/shard_map/all_to_all | solution.py:326
  80.6 3.5 %collective-permute-start.2 = (bf16[8,144,128]{2,1,0:T(8,128)(2,1)S(1)}, bf16[8,144,128]{2,1,0:T(8,128)(2,1)S(1)}, u32[]{:S(2)}, u32[]{:S(2)}) collective-permute-start(bf16[8,144,128]{2,1,0:T(8,128)(2,1)S(1)} %get-tuple-element.35), channel_id=1, source_target_pairs={{0,1},{1,0},{2,3},{3,2},{4,5},{5,4},{6,7},{7,6},{8,9},{9,8},{10,11... | collective-permute-start | bytes 884744 | tf_op jit(solution)/shard_map/ppermute | solution.py:330
